TPU v7x, 128 devices: a whole 4x4x4 slice. The times are simulated.
128 devices in a mesh: rep: 1, seq: 128 (over z, y, x, core).
Axes of the slice: x: 4, y: 4, z: 4, core: 2. Of those that a mesh axis runs over, the one named last changes fastest.
Arguments:
- hidden: bfloat16 [16, 8192], P('rep')
- w_query: bfloat16 [8192, 8192], replicated
- w_key: bfloat16 [8192, 1024], replicated
- w_value: bfloat16 [8192, 1024], replicated
- w_out: bfloat16 [8192, 8192], P('seq')
- k_cache: bfloat16 [16, 8192, 8, 128], P('rep', 'seq')
- v_cache: bfloat16 [16, 8192, 8, 128], P('rep', 'seq')
- positions: int32 [16], P('rep')
Outputs:
- output 1: bfloat16 [16, 8192], P('rep')
- output 2: bfloat16 [16, 8192, 8, 128], P('rep', 'seq')
- output 3: bfloat16 [16, 8192, 8, 128], P('rep', 'seq')
All inputs are finite; a program needn't handle non-finite values.
Results may differ from a plain program's by a relative error of at most 0.0046317.
Values are sent between devices in bfloat16 or wider.
A program may use at most 1 GiB of HBM per device.

v0:
```python
import jax
import jax.numpy as jnp
from jax import lax
from jax.sharding import PartitionSpec as P


def solution(mesh):
    cache_spec = P('rep', 'seq', None, None)
    in_specs = (P('rep', None), P(), P(), P(), P('seq', None), cache_spec, cache_spec, P('rep'))
    out_specs = (P('rep', None), cache_spec, cache_spec)

    def local_step(hidden, w_query, w_key, w_value, w_out, k_cache, v_cache, positions):
        batch_size, local_len, kv_heads, head_dim = k_cache.shape
        num_heads = w_query.shape[1] // head_dim
        group_size = num_heads // kv_heads
        shard_idx = lax.axis_index('seq')
        q_flat = jnp.dot(hidden, w_query, preferred_element_type=jnp.float32).astype(jnp.bfloat16)
        key_new = jnp.dot(hidden, w_key, preferred_element_type=jnp.float32).astype(jnp.bfloat16).reshape(batch_size, kv_heads, head_dim)
        value_new = jnp.dot(hidden, w_value, preferred_element_type=jnp.float32).astype(jnp.bfloat16).reshape(batch_size, kv_heads, head_dim)
        seq_ids = shard_idx * local_len + jnp.arange(local_len)
        at_pos = (seq_ids[None, :] == positions[:, None])[:, :, None, None]
        k_updated = jnp.where(at_pos, key_new[:, None], k_cache)
        v_updated = jnp.where(at_pos, value_new[:, None], v_cache)
        is_valid = (seq_ids[None, :] <= positions[:, None])[:, None, None, :]
        q_heads = q_flat.reshape(batch_size, kv_heads, group_size, head_dim)
        scores = jnp.einsum('bkgd,bskd->bkgs', q_heads, k_updated, preferred_element_type=jnp.float32) * head_dim ** -0.5
        scores = jnp.where(is_valid, scores, -jnp.inf)
        local_max = jnp.max(scores, axis=-1)
        safe_max = jnp.where(jnp.isfinite(local_max), local_max, 0.0)
        weights = jnp.exp(scores - safe_max[..., None])
        local_sum = jnp.sum(weights, axis=-1)
        local_out = jnp.einsum('bkgs,bskd->bkgd', weights.astype(jnp.bfloat16), v_updated, preferred_element_type=jnp.float32)
        global_max = lax.pmax(local_max, 'seq')
        rescale = jnp.exp(local_max - global_max)
        total_sum, total_out = lax.psum((local_sum * rescale, local_out * rescale[..., None]), 'seq')
        combined = (total_out / total_sum[..., None]).astype(jnp.bfloat16).reshape(batch_size, num_heads * head_dim)
        row_count = w_out.shape[0]
        combined_rows = lax.dynamic_slice_in_dim(combined, shard_idx * row_count, row_count, axis=1)
        part_out = jnp.dot(combined_rows, w_out, preferred_element_type=jnp.float32)
        result = lax.psum(part_out, 'seq').astype(jnp.bfloat16)
        return result, k_updated, v_updated

    return jax.shard_map(local_step, mesh=mesh, in_specs=in_specs, out_specs=out_specs, check_vma=False)
```

profile of v0, /device:TPU:1, one launch (start us, length us, event | category | flops | bytes accessed | tf_op | source)
XLA Modules:
  0.0 366.7 jit_solution(7120158284145298495)
XLA Ops:
  7.2 0.0 copy-start
  7.2 0.0 all-reduce.3.cloned.1.call-start
  7.2 0.0 copy-start.1
  7.3 0.0 copy-start.3
  7.3 8.3 %fusion.14 = bf16[2,8,8,128]{3,1,2,0:T(8,128)(2,1)S(1)} fusion(bf16[16,8192]{1,0:T(8,128)(2,1)} %param.8, bf16[8192,1024]{1,0:T(8,128)(2,1)} %param.10), kind=kOutput, calls=%fused_computation.13 | convolution fusion | flops 268451840 | bytes 17072128 | tf_op jit(solution)/shard_map/dot_general | solution.py:18
  15.6 2.4 copy-done.1
  17.9 0.0 copy-done.3
  17.9 2.3 fusion.15
  20.2 0.0 copy-start.4
  20.3 43.4 %fusion.13 = bf16[2,8,64,128]{3,1,2,0:T(8,128)(2,1)S(1)} fusion(bf16[16,8192]{1,0:T(8,128)(2,1)S(1)} %copy-done.3, bf16[8192,8192]{1,0:T(8,128)(2,1)} %param.9), kind=kOutput, calls=%fused_computation.10 | convolution fusion | flops 2147614720 | bytes 134742016 | tf_op jit(solution)/shard_map/dot_general | solution.py:17
  63.7 0.0 copy-done.4
  63.7 0.1 broadcast_compare_fusion.1
  63.8 4.8 %broadcast_select_fusion.1 = (bf16[16,64,8,128]{3,2,1,0:T(8,128)(2,1)S(1)}, bf16[16,64,8,128]{3,2,1,0:T(8,128)(2,1)}) fusion(bf16[16,64,8,128]{3,2,1,0:T(8,128)(2,1)} %param.13, pred[16,64]{1,0:T(8,128)(4,1)S(1)} %get-tuple-element.8, bf16[16,8,128]{2,1,0:T(8,128)(2,1)S(1)} %bitcast.26, bf16[16,64,8,128]{3,2,1,0:T(8,128)(2,1)} %param.14, ...), kind=kLoop, calls=%fused_computation.6 | loop fusion | flops 2097152 | bytes 8455168 | tf_op jit(solution)/shard_map/jit(_where)/select_n | solution.py:22
  68.5 0.0 copy-start.2
  68.5 2.0 fusion.24
  70.5 69.1 %pmax.7 = f32[16,8,8]{2,1,0:T(8,128)S(1)} all-reduce(f32[16,8,8]{2,1,0:T(8,128)S(1)} %get-tuple-element.9), channel_id=1, replica_groups=mesh['rep'=1,'seq'=128] {'seq'}, use_global_device_ids=true, to_apply=%region_1.2 | all-reduce | flops 1024 | bytes 8192 | tf_op jit(solution)/shard_map/pmax | solution.py:33
  139.7 1.4 fusion.16
  141.1 0.0 copy-done.2
  141.1 3.3 fusion.10
  144.4 0.0 all-reduce.3.cloned.1.call-update
  144.5 62.8 %psum.22 = f32[16,8,8]{2,1,0:T(8,128)S(1)} all-reduce(f32[16,8,8]{2,1,0:T(8,128)S(1)} %get-tuple-element.3), channel_id=1, replica_groups=mesh['rep'=1,'seq'=128] {'seq'}, use_global_device_ids=true, to_apply=%region_4.5 | all-reduce | flops 1024 | bytes 8192 | tf_op jit(solution)/shard_map/psum | solution.py:35
  207.2 82.6 %all-reduce.3.cloned.1.call-done = f32[16,8,8,128]{3,2,1,0:T(8,128)} async-done(((f32[16,8,8,128]{3,2,1,0:T(8,128)}), f32[16,8,8,128]{3,2,1,0:T(8,128)}) %all-reduce.3.cloned.1.call-update) | async-done | bytes 524304 | tf_op jit(solution)/shard_map/psum | solution.py:35
  289.9 1.2 divide_convert_fusion
  291.1 0.2 copy.30
  291.3 0.0 copy-done
  291.3 0.3 fusion.20
  291.6 68.2 %all-reduce.4 = bf16[16,8192]{1,0:T(8,128)(2,1)} all-reduce(f32[16,8192]{1,0:T(8,128)S(1)} %fusion.20), channel_id=1, replica_groups=mesh['rep'=1,'seq'=128] {'seq'}, use_global_device_ids=true, to_apply=%region_5.6 | all-reduce | flops 131072 | bytes 786432 | tf_op jit(solution)/shard_map/psum | solution.py:40
  (6 shorter events, 0.1 us)
Async XLA Ops:
  7.2 284.1 %copy-start = (bf16[64,8192]{1,0:T(8,128)(2,1)S(1)}, bf16[64,8192]{1,0:T(8,128)(2,1)}, u32[]{:S(2)}) copy-start(bf16[64,8192]{1,0:T(8,128)(2,1)} %param.12) | copy-start | bytes 3145732
  7.2 282.7 %all-reduce.3.cloned.1.call-start = ((), (), s32[]{:S(2)}) async-start(), calls=%async_computation | async-start | bytes 1048576 | tf_op jit(solution)/shard_map/psum | solution.py:35
  7.2 10.7 %copy-start.1 = (bf16[8192,1024]{1,0:T(8,128)(2,1)S(1)}, bf16[8192,1024]{1,0:T(8,128)(2,1)}, u32[]{:S(2)}) copy-start(bf16[8192,1024]{1,0:T(8,128)(2,1)} %param.11) | copy-start | bytes 50331652
  7.3 10.7 %copy-start.3 = (bf16[16,8192]{1,0:T(8,128)(2,1)S(1)}, bf16[16,8192]{1,0:T(8,128)(2,1)}, u32[]{:S(2)}) copy-start(bf16[16,8192]{1,0:T(8,128)(2,1)} %param.8) | copy-start | bytes 786436
  20.2 43.4 %copy-start.4 = (s32[16]{0:T(128)S(1)}, s32[16]{0:T(128)}, u32[]{:S(2)}) copy-start(s32[16]{0:T(128)} %param.15) | copy-start | bytes 196
  68.5 72.6 %copy-start.2 = (bf16[16,64,8,128]{3,2,1,0:T(8,128)(2,1)}, bf16[16,64,8,128]{3,2,1,0:T(8,128)(2,1)S(1)}, u32[]{:S(2)}) copy-start(bf16[16,64,8,128]{3,2,1,0:T(8,128)(2,1)S(1)} %get-tuple-element.5) | copy-start | bytes 6291460
Sparse Core Ops, SparseCore 0:
  144.6 145.2 all-reduce.2
where the time goes:
time: 367 us
  blocking collectives  200 us (54%)
  waiting for transfers between devices  82.7 us (23%)
  matrix products  59.5 us (16%)
  between operations  14.2 us (4%)
  other arithmetic  7.54 us (2%)
    psum x1, waiting for transfers between devices, local_step(): lax.psum((local_sum * rescale, local_out * rescale[..., None]), 'seq')  82.6 us
    pmax x1, blocking collectives, local_step(): global_max = lax.pmax(local_max, 'seq')  69.1 us
    psum x1, blocking collectives, local_step(): result = lax.psum(part_out, 'seq').astype(jnp.bfloat16)  68.2 us
    psum x1, blocking collectives, local_step(): lax.psum((local_sum * rescale, local_out * rescale[..., None]), 'seq')  62.8 us
    dot_general x1, matrix products, local_step(): jnp.dot(hidden, w_query, preferred_element_type=jnp.float32)  43.4 us
    dot_general x1, matrix products, local_step(): jnp.dot(hidden, w_key, preferred_element_type=jnp.float32)  8.27 us
  transfers between devices with their start and end apart: 1, of which 1 were waited for; matrix products, arithmetic and copies ran while one was open for 0% of the time, Pallas kernels for 0%

commit v1 on v0

v1 whole, which is shorter than its diff:
```python
import functools
import jax
import jax.numpy as jnp
from jax import lax
from jax.experimental import pallas as pl
from jax.experimental.pallas import tpu as pltpu
from jax.sharding import PartitionSpec as P

BF16 = jnp.bfloat16
F32 = jnp.float32
MESH = pl.DeviceIdType.MESH
KCH = 8
RING = (0, 1, 2, 1)


def offsets():
    offs = [(dz, dy, dx) for dz in range(4) for dy in range(4) for dx in range(4)][1:]
    return sorted(offs, key=lambda o: -(RING[o[0]] + RING[o[1]] + RING[o[2]]))


def main_kernel(pos_ref, x_ref, wq_ref, wk_ref, wv_ref, wo_ref, k_ref, v_ref,
                y_ref, kvnew_ref,
                wqb, wkvb, kbuf, vbuf, wob, qsend, qrecv, kvsend, kvrecv, kvf, qf, colidx,
                osend, orecv, ssend, srecv, ysend, yrecv, yb, yg,
                wsem, ksem, d2d_send, d2d_recv, q_send, q_recv, o_send, o_recv,
                s_send, s_recv, ys_send, ys_recv, yg_send, yg_recv, pp_send, pp_recv):
    me = lax.axis_index("seq")
    chip, core = me // 2, me % 2
    cx, cy, cz = chip % 4, (chip // 4) % 4, chip // 16
    other = 1 - core
    cube = (cz % 2) * 4 + (cy % 2) * 2 + (cx % 2)
    bz, by, bx = cz - cz % 2, cy - cy % 2, cx - cx % 2
    slot = cube * 2 + core

    def dev(d):
        return {"seq": d}

    def chip_at(o):
        return ((cz + o[0]) % 4) * 16 + ((cy + o[1]) % 4) * 4 + (cx + o[2]) % 4

    def cube_chip(o):
        t = (cube + o) % 8
        return (bz + t // 4) * 16 + (by + (t // 2) % 2) * 4 + bx + t % 2

    rows = 8192 // KCH
    qcol = pl.multiple_of(slot * 512, 512)
    kcol = pl.multiple_of(cube * 128, 128)

    def wq_copy(i):
        return pltpu.make_async_copy(wq_ref.at[pl.ds(i * rows, rows), pl.ds(qcol, 512)],
                                     wqb.at[pl.ds(i * rows, rows)], wsem.at[i])

    def wkv_copy(ref, i):
        return pltpu.make_async_copy(ref.at[pl.ds(i * rows, rows), pl.ds(kcol, 128)],
                                     wkvb.at[pl.ds(i * rows, rows)], wsem.at[KCH + i])

    for i in range(KCH):
        wq_copy(i).start()

    @pl.when(core == 0)
    def _():
        for i in range(KCH):
            wkv_copy(wk_ref, i).start()

    @pl.when(core == 1)
    def _():
        for i in range(KCH):
            wkv_copy(wv_ref, i).start()

    mine = pl.multiple_of(core * 8, 8)
    theirs = pl.multiple_of(other * 8, 8)
    loc = [pltpu.make_async_copy(k_ref.at[pl.ds(mine, 8)], kbuf.at[:, core], ksem.at[0]),
           pltpu.make_async_copy(v_ref.at[pl.ds(mine, 8)], vbuf.at[:, core], ksem.at[1]),
           pltpu.make_async_copy(wo_ref, wob.at[core], ksem.at[2])]
    for c in loc:
        c.start()

    bar = pltpu.get_barrier_semaphore()
    partner = chip * 2 + other
    for o in offsets():
        pl.semaphore_signal(bar, inc=1, device_id=dev(chip_at(o) * 2 + core), device_id_type=MESH)
    for o in range(8):
        pl.semaphore_signal(bar, inc=1, device_id=dev(cube_chip(o) * 2 + other), device_id_type=MESH)

    col = lax.broadcasted_iota(jnp.int32, (64, 1024), 1)
    row = lax.broadcasted_iota(jnp.int32, (64, 1024), 0)
    colidx[...] = jnp.where(col % 8 == row // 8, chip * 128 + col // 8, 1 << 30)

    accq = jnp.zeros((16, 512), F32)
    for i in range(KCH):
        wq_copy(i).wait()
        accq = accq + jnp.dot(x_ref[:, i * rows:(i + 1) * rows], wqb[i * rows:(i + 1) * rows, :],
                              preferred_element_type=F32)
    for h in range(2):
        qsend[h] = accq[h * 8:h * 8 + 8].astype(BF16)
    acck = jnp.zeros((16, 128), F32)
    for i in range(KCH):
        wkv_copy(wk_ref, i).wait()
        acck = acck + jnp.dot(x_ref[:, i * rows:(i + 1) * rows], wkvb[i * rows:(i + 1) * rows, :],
                              preferred_element_type=F32)
    for h in range(2):
        kvsend[h] = acck[h * 8:h * 8 + 8].astype(BF16)
    pl.semaphore_wait(bar, 71)

    def rcopy(src, dst, ss, rs, d):
        return pltpu.make_async_remote_copy(src_ref=src, dst_ref=dst, send_sem=ss, recv_sem=rs,
                                            device_id=dev(d), device_id_type=MESH)

    targets = [(cube_chip(o), 0) for o in (7, 6, 5, 3, 4, 2, 1)]
    for ch, _ in targets:
        for c2 in (core, other):
            rcopy(qsend.at[c2], qrecv.at[slot], q_send.at[0], q_recv.at[0], ch * 2 + c2).start()
    rcopy(qsend.at[other], qrecv.at[slot], q_send.at[0], q_recv.at[0], partner).start()
    for ch, _ in targets:
        for c2 in (core, other):
            rcopy(kvsend, kvrecv.at[core * 8 + cube], q_send.at[1], q_recv.at[1], ch * 2 + c2).start()
    rcopy(kvsend, kvrecv.at[core * 8 + cube], q_send.at[1], q_recv.at[1], partner).start()
    dd = [rcopy(k_ref.at[pl.ds(theirs, 8)], kbuf.at[:, core], d2d_send.at[0], d2d_recv.at[0], partner),
          rcopy(v_ref.at[pl.ds(theirs, 8)], vbuf.at[:, core], d2d_send.at[1], d2d_recv.at[1], partner),
          rcopy(wo_ref, wob.at[core], d2d_send.at[2], d2d_recv.at[2], partner)]
    for c in dd:
        c.start()
    qrecv[slot] = qsend[core]
    kvrecv[core * 8 + cube] = kvsend[...]

    def wait_all(ref, sem):
        pltpu.make_async_copy(ref, ref, sem).wait()

    wait_all(qrecv.at[pl.ds(0, 15)], q_recv.at[0])
    for s in range(16):
        q8 = qrecv[s].astype(F32)
        for j in range(4):
            qf[:, s * 4 + j, :] = q8[:, j * 128:(j + 1) * 128]
    wait_all(kvrecv.at[pl.ds(0, 15)], q_recv.at[1])
    for kv in range(2):
        for h in range(8):
            for half in range(2):
                kvf[kv, half, :, h, :] = kvrecv[kv * 8 + h, half].astype(F32)
    kvnew_ref[...] = kvf[...].astype(BF16)
    loc[0].wait()
    loc[1].wait()
    dd[0].wait_recv()
    dd[1].wait_recv()

    lane = lax.broadcasted_iota(jnp.int32, (64, 128), 1)
    stats = jnp.zeros((64, 128), F32)
    scale = 128 ** -0.5
    neg = -jnp.inf
    for b in range(8):
        pos = pos_ref[core * 8 + b]
        qb = qf[b]
        kn = jnp.broadcast_to(kvf[0, core, b][:, None, :], (8, 8, 128)).reshape(64, 128)
        vn = jnp.broadcast_to(kvf[1, core, b][:, None, :], (8, 8, 128)).reshape(64, 128)
        s = lax.dot_general(qb.astype(BF16), kbuf[b].reshape(1024, 128), (((1,), (1,)), ((), ())),
                            preferred_element_type=F32) * scale
        s = jnp.where(colidx[...] < pos, s, neg)
        snew = jnp.sum(qb * kn, axis=1, keepdims=True) * scale
        here = jnp.full((64, 1), pos // 128, jnp.int32) == chip
        snew = jnp.where(here, snew, neg)
        m = jnp.maximum(jnp.max(s, axis=1, keepdims=True), snew)
        msafe = jnp.where(m == neg, 0.0, m)
        p = jnp.exp(s - msafe)
        pn = jnp.exp(snew - msafe)
        l = jnp.sum(p, axis=1, keepdims=True) + pn
        o = jnp.dot(p.astype(BF16), vbuf[b].reshape(1024, 128), preferred_element_type=F32) + pn * vn
        osend[:, b, :] = o
        stats = jnp.where(lane == b, m, stats)
        stats = jnp.where(lane == 8 + b, l, stats)
    ssend[:, 0, :] = stats

    for o in offsets():
        d = chip_at(o)
        rcopy(osend.at[d], orecv.at[chip], o_send, o_recv, d * 2 + core).start()
        rcopy(ssend.at[d], srecv.at[chip], s_send, s_recv, d * 2 + core).start()
    orecv[chip] = osend[chip]
    srecv[chip] = ssend[chip]
    loc[2].wait()
    dd[2].wait_recv()
    wait_all(srecv.at[pl.ds(0, 63)], s_recv)
    st = jnp.concatenate([srecv[:, 0, :], jnp.zeros((64, 128), F32)], axis=0).T
    mt = st[0:8, 0:64]
    lt = st[8:16, 0:64]
    mx = jnp.max(mt, axis=1, keepdims=True)
    w = jnp.exp(mt - mx)
    tot = jnp.sum(w * lt, axis=1, keepdims=True)
    wait_all(orecv.at[pl.ds(0, 63)], o_recv)
    acc = jnp.zeros((8, 128), F32)
    for i in range(64):
        acc = acc + w[:, i:i + 1] * orecv[i]
    ob = (acc / tot).astype(BF16)

    for j in range(16):
        wj = wob[:, :, j * 512:(j + 1) * 512].reshape(128, 512)
        part = jnp.dot(ob, wj, preferred_element_type=F32)
        for jj in range(4):
            ysend[j * 4 + jj] = part[:, jj * 128:(jj + 1) * 128]
    for o in offsets():
        d = chip_at(o)
        rcopy(ysend.at[d], yrecv.at[chip], ys_send, ys_recv, d * 2 + core).start()
    yrecv[chip] = ysend[chip]
    wait_all(yrecv.at[pl.ds(0, 63)], ys_recv)
    acc = yrecv[0]
    for i in range(1, 64):
        acc = acc + yrecv[i]
    yb[...] = acc.astype(BF16)

    for o in offsets():
        rcopy(yb, yg.at[core, chip], yg_send, yg_recv, chip_at(o) * 2 + core).start()
    yg[core, chip] = yb[...]
    wait_all(yg.at[0, pl.ds(0, 63)], yg_recv)
    fwd = rcopy(yg.at[core], yg.at[core], pp_send, pp_recv, partner)
    fwd.start()
    y_ref[core] = yg[core]
    fwd.wait_recv()
    y_ref[other] = yg[other]

    fwd.wait_send()
    wait_all(yg.at[0, pl.ds(0, 63)], yg_send)
    wait_all(yrecv.at[pl.ds(0, 63)], ys_send)
    wait_all(orecv.at[pl.ds(0, 63)], o_send)
    wait_all(srecv.at[pl.ds(0, 63)], s_send)
    wait_all(qrecv.at[pl.ds(0, 15)], q_send.at[0])
    wait_all(kvrecv.at[pl.ds(0, 15)], q_send.at[1])
    for c in dd:
        c.wait_send()


def update_kernel(pos_ref, new_ref, k_ref, v_ref, ko_ref, vo_ref, buf, isem, osem):
    me = lax.axis_index("seq")
    base = me * 64
    n = 8
    srcs, dsts = (k_ref, v_ref), (ko_ref, vo_ref)

    def rd(t, i):
        return pltpu.make_async_copy(srcs[t].at[pl.ds(i * 2, 2)], buf.at[t, pl.ds(i * 2, 2)], isem.at[t, i])

    def wr(t, i):
        return pltpu.make_async_copy(buf.at[t, pl.ds(i * 2, 2)], dsts[t].at[pl.ds(i * 2, 2)], osem.at[t, i])

    for i in range(n):
        for t in range(2):
            rd(t, i).start()
    for i in range(n):
        for t in range(2):
            rd(t, i).wait()
            for b in (2 * i, 2 * i + 1):
                r = pos_ref[b] - base

                @pl.when((r >= 0) & (r < 64))
                def _():
                    buf[t, b, r] = new_ref[t, b]
            wr(t, i).start()
    for i in range(n):
        for t in range(2):
            wr(t, i).wait()


def solution(mesh):
    cache_spec = P('rep', 'seq', None, None)
    in_specs = (P('rep', None), P(), P(), P(), P('seq', None), cache_spec, cache_spec, P('rep'))
    out_specs = (P('rep', None), cache_spec, cache_spec)
    vmem, anyspace, smem = (pl.BlockSpec(memory_space=s) for s in (pltpu.VMEM, pl.ANY, pltpu.SMEM))
    dma = pltpu.SemaphoreType.DMA

    def local_step(x, wq, wk, wv, wo, k, v, pos):
        y, new = pl.pallas_call(
            main_kernel,
            name="decode",
            out_shape=(jax.ShapeDtypeStruct((2, 64, 8, 128), BF16),
                       jax.ShapeDtypeStruct((2, 2, 8, 8, 128), BF16)),
            in_specs=[smem, vmem] + [anyspace] * 6,
            out_specs=(vmem, vmem),
            scratch_shapes=[
                pltpu.VMEM((8192, 512), BF16), pltpu.VMEM((8192, 128), BF16),
                pltpu.VMEM((8, 2, 512, 128), BF16), pltpu.VMEM((8, 2, 512, 128), BF16),
                pltpu.VMEM((2, 64, 8192), BF16),
                pltpu.VMEM((2, 8, 512), BF16), pltpu.VMEM((16, 8, 512), BF16),
                pltpu.VMEM((2, 8, 128), BF16), pltpu.VMEM((16, 2, 8, 128), BF16),
                pltpu.VMEM((2, 2, 8, 8, 128), F32), pltpu.VMEM((8, 64, 128), F32),
                pltpu.VMEM((64, 1024), jnp.int32),
                pltpu.VMEM((64, 8, 128), F32), pltpu.VMEM((64, 8, 128), F32),
                pltpu.VMEM((64, 1, 128), F32), pltpu.VMEM((64, 1, 128), F32),
                pltpu.VMEM((64, 8, 128), F32), pltpu.VMEM((64, 8, 128), F32),
                pltpu.VMEM((8, 128), BF16), pltpu.VMEM((2, 64, 8, 128), BF16),
                dma((2 * KCH,)), dma((3,)), dma((3,)), dma((3,)), dma((2,)), dma((2,)),
                dma, dma, dma, dma, dma, dma, dma, dma, dma, dma,
            ],
            compiler_params=pltpu.CompilerParams(collective_id=0, has_side_effects=True,
                                                 vmem_limit_bytes=60 << 20),
        )(pos, x, wq, wk, wv, wo, k.reshape(16, 512, 128), v.reshape(16, 512, 128))
        result = y.transpose(0, 2, 1, 3).reshape(16, 8192)
        ko, vo = pl.pallas_call(
            update_kernel,
            name="update",
            out_shape=(jax.ShapeDtypeStruct(k.shape, BF16),) * 2,
            in_specs=[smem, vmem, anyspace, anyspace],
            out_specs=(anyspace, anyspace),
            scratch_shapes=[pltpu.VMEM((2, 16, 64, 8, 128), BF16), dma((2, 8)), dma((2, 8))],
            compiler_params=pltpu.CompilerParams(vmem_limit_bytes=32 << 20),
        )(pos, new.reshape(2, 16, 8, 128), k, v)
        return result, ko, vo

    return jax.shard_map(local_step, mesh=mesh, in_specs=in_specs, out_specs=out_specs, check_vma=False)
```

time: 367 us -> 49.4 us (0.13)
  blocking collectives: 200 us -> 0 us
  waiting for transfers between devices: 82.7 us -> 0 us
  matrix products: 59.5 us -> 0 us
  Pallas kernels: 0 us -> 45.4 us
  between operations: 14.2 us -> 0.7 us
  other arithmetic: 7.54 us -> 0 us
    psum x2 -> x0, blocking collectives: 131 us -> none  [the longest x1 68.2 us: local_step(): result = lax.psum(part_out, 'seq').astype(jnp.bfloat16)]
    psum x1 -> x0, waiting for transfers between devices: 82.6 us -> none  [local_step(): lax.psum((local_sum * rescale, local_out * rescale[..., None]), 'seq')]
    pmax x1 -> x0, blocking collectives: 69.1 us -> none  [local_step(): global_max = lax.pmax(local_max, 'seq')]
    dot_general x6 -> x0, matrix products: 59.5 us -> none  [the longest x1 43.4 us: local_step(): jnp.dot(hidden, w_query, preferred_element_type=jnp.float32)]
    pallas_call x0 -> x2, Pallas kernels: none -> 45.4 us  [the longest x1 42.3 us: local_step(): pl.pallas_call(main_kernel, name='decode', out_shape=(jax.ShapeDtypeStruc...]
    select_n x2 -> x0, other arithmetic: 4.76 us -> none  [the longest x1 4.75 us: local_step(): k_updated = jnp.where(at_pos, key_new[:, None], k_cache)]
  transfers between devices with their start and end apart: 1 -> 0, of which waited for: 1 -> 0; matrix products, arithmetic and copies ran while one was open for 0% -> 0% of each run, Pallas kernels for 0% -> 0%
where the time goes in v1:
time: 49.4 us; the launch traced here: 49.2 us
  Pallas kernels  45.4 us (92%)
  local copies, waits for them, and re-layouts  3.14 us (6%)
  between operations  0.7 us (1%)
    pallas_call x1, Pallas kernels, local_step(): pl.pallas_call(main_kernel, name='decode', out_shape=(jax.ShapeDtypeStruc...  42.3 us
    unnamed x11, local copies, waits for them, and re-layouts  3.14 us
    pallas_call x1, Pallas kernels, local_step(): pl.pallas_call(update_kernel, name='update', out_shape=(jax.ShapeDtypeStr...  3.14 us

profile of v1, /device:TPU:1, one launch (start us, length us, event | category | flops | bytes accessed | tf_op | source)
XLA Modules:
  0.0 49.2 jit_solution(3838973192418642782)
XLA Ops:
  0.6 0.0 copy-start
  0.6 0.0 copy-start.3
  0.7 42.3 %decode.1 = (bf16[2,64,8,128]{3,2,1,0:T(8,128)(2,1)}, bf16[2,2,8,8,128]{4,3,2,1,0:T(8,128)(2,1)}) custom-call(s32[16]{0:T(128)} %pos_ref.3, bf16[16,8192]{1,0:T(8,128)(2,1)} %x_ref.1, bf16[8192,8192]{1,0:T(8,128)(2,1)} %wq_ref.1, bf16[8192,1024]{1,0:T(8,128)(2,1)} %wk_ref.1, bf16[8192,1024]{1,0:T(8,128)(2,1)} %wv_ref.1, bf16[64,8192]{1,0:T(8,128)(2,1)} %wo_ref.1, ...), custom_call_target="tpu_custom_call" | custom-call | tf_op jit(solution)/shard_map/decode/pallas_call | solution.py:266
  42.9 0.0 copy-done
  42.9 0.0 copy-done.3
  42.9 0.0 copy-start.1
  43.0 1.6 %copy-done.1 = bf16[16,64,8,128]{3,2,1,0:T(8,128)(2,1)S(1)} copy-done((bf16[16,64,8,128]{3,2,1,0:T(8,128)(2,1)S(1)}, bf16[16,64,8,128]{3,2,1,0:T(8,128)(2,1)}, u32[]{:S(2)}) %copy-start.1) | copy-done | bytes 2097176
  44.5 0.0 copy-start.2
  44.5 0.8 %copy-done.2 = bf16[2,2,8,8,128]{4,3,2,1,0:T(8,128)(2,1)S(1)} copy-done((bf16[2,2,8,8,128]{4,3,2,1,0:T(8,128)(2,1)S(1)}, bf16[2,2,8,8,128]{4,3,2,1,0:T(8,128)(2,1)}, u32[]{:S(2)}) %copy-start.2) | copy-done | bytes 65560
  45.4 0.0 copy-start.4
  45.4 3.1 %update.1 = (bf16[16,64,8,128]{3,2,1,0:T(8,128)(2,1)}, bf16[16,64,8,128]{3,2,1,0:T(8,128)(2,1)}) custom-call(s32[16]{0:T(128)S(1)} %copy-done.3, bf16[2,16,8,128]{3,2,1,0:T(8,128)(2,1)S(1)} %bitcast.8, bf16[16,64,8,128]{3,2,1,0:T(8,128)(2,1)S(1)} %copy-done, bf16[16,64,8,128]{3,2,1,0:T(8,128)(2,1)S(1)} %copy-done.1), custom_call_target="tpu_custom_call" | custom-call | tf_op jit(solution)/shard_map/update/pallas_call | solution.py:292
  48.5 0.0 copy-done.4
  48.5 0.7 %copy.12 = bf16[16,8192]{1,0:T(8,128)(2,1)} copy(bf16[16,8192]{1,0:T(8,128)(2,1)S(1)} %bitcast.9) | data formatting | bytes 524288
Async XLA Ops:
  0.6 42.3 %copy-start = (bf16[16,64,8,128]{3,2,1,0:T(8,128)(2,1)S(1)}, bf16[16,64,8,128]{3,2,1,0:T(8,128)(2,1)}, u32[]{:S(2)}) copy-start(bf16[16,64,8,128]{3,2,1,0:T(8,128)(2,1)} %k_ref.1) | copy-start | bytes 6291460
  0.6 42.3 %copy-start.3 = (s32[16]{0:T(128)S(1)}, s32[16]{0:T(128)}, u32[]{:S(2)}) copy-start(s32[16]{0:T(128)} %pos_ref.3) | copy-start | bytes 196
  42.9 1.6 %copy-start.1 = (bf16[16,64,8,128]{3,2,1,0:T(8,128)(2,1)S(1)}, bf16[16,64,8,128]{3,2,1,0:T(8,128)(2,1)}, u32[]{:S(2)}) copy-start(bf16[16,64,8,128]{3,2,1,0:T(8,128)(2,1)} %v_ref.1) | copy-start | bytes 6291460
  44.5 0.8 %copy-start.2 = (bf16[2,2,8,8,128]{4,3,2,1,0:T(8,128)(2,1)S(1)}, bf16[2,2,8,8,128]{4,3,2,1,0:T(8,128)(2,1)}, u32[]{:S(2)}) copy-start(bf16[2,2,8,8,128]{4,3,2,1,0:T(8,128)(2,1)} %get-tuple-element.8) | copy-start | bytes 196612
  45.4 3.1 %copy-start.4 = (bf16[2,64,8,128]{3,2,1,0:T(8,128)(2,1)S(1)}, bf16[2,64,8,128]{3,2,1,0:T(8,128)(2,1)}, u32[]{:S(2)}) copy-start(bf16[2,64,8,128]{3,2,1,0:T(8,128)(2,1)} %get-tuple-element.7) | copy-start | bytes 786436

commit v2 on v1

v2 whole, which is shorter than its diff:
```python
import functools
import jax
import jax.numpy as jnp
from jax import lax
from jax.experimental import pallas as pl
from jax.experimental.pallas import tpu as pltpu
from jax.sharding import PartitionSpec as P

BF16 = jnp.bfloat16
F32 = jnp.float32
MESH = pl.DeviceIdType.MESH
DECODE_VMEM = 40
KCH = 8
RING = (0, 1, 2, 1)


def offsets():
    offs = [(dz, dy, dx) for dz in range(4) for dy in range(4) for dx in range(4)][1:]
    return sorted(offs, key=lambda o: -(RING[o[0]] + RING[o[1]] + RING[o[2]]))


def hops(o):
    return RING[o[0]] + RING[o[1]] + RING[o[2]]


def colour_offsets():
    best = {}
    for o in sorted(offsets(), key=lambda o: (hops(o), o)):
        d = ((o[2] + o[0]) % 4, (o[1] + o[0]) % 4)
        neg = ((-d[0]) % 4, (-d[1]) % 4)
        if d == (0, 0) or d in best or (d == neg and any(c % 2 for c in o)):
            continue
        best[d] = o
        best[neg] = tuple(-c % 4 for c in o)
    return sorted(best.values(), key=lambda o: -hops(o))


NEAR = [z * 16 + y * 4 + x for z in range(4) for y in range(4) for x in range(4) if hops((z, y, x)) <= 1]


def start_distance(chip):
    ring = lambda c: jnp.where(c == 3, 1, c)
    return ring(chip % 4) + ring((chip // 4) % 4) + ring(chip // 16)


def main_kernel(pos_hbm, x_hbm, wq_ref, wk_ref, wv_ref, wo_ref, k_ref, v_ref,
                y_ref, kvnew_ref,
                pos_ref, x_ref, khalf, vhalf, wqb, wkvb, kbuf, vbuf, wob, qsend, qrecv, kvsend, kvrecv, kvf, qf, colidx,
                osend, orecv, ssend, srecv, ysend, yrecv, yb, yg,
                xsem, wsem, ksem, d2d_send, d2d_recv, q_send, q_recv, o_send, o_recv,
                s_send, s_recv, ys_send, ys_recv, yg_send, yg_recv, pp_send, pp_recv, pn_send, pn_recv):
    me = lax.axis_index("seq")
    chip, core = me // 2, me % 2
    cx, cy, cz = chip % 4, (chip // 4) % 4, chip // 16
    other = 1 - core
    colour = ((cx + cz) % 4) * 4 + (cy + cz) % 4
    slot = colour * 2 + core

    def dev(d):
        return {"seq": d}

    def chip_at(o):
        return ((cz + o[0]) % 4) * 16 + ((cy + o[1]) % 4) * 4 + (cx + o[2]) % 4

    rows = 8192 // KCH
    qcol = pl.multiple_of(slot * 256, 256)
    kcol = pl.multiple_of((colour % 8) * 128, 128)

    def wq_copy(i):
        return pltpu.make_async_copy(wq_ref.at[pl.ds(i * rows, rows), pl.ds(qcol, 256)],
                                     wqb.at[pl.ds(i * rows, rows)], wsem.at[i])

    def wkv_copy(ref, i):
        return pltpu.make_async_copy(ref.at[pl.ds(i * rows, rows), pl.ds(kcol, 128)],
                                     wkvb.at[pl.ds(i * rows, rows)], wsem.at[KCH + i])

    xload = [pltpu.make_async_copy(x_hbm, x_ref, xsem.at[0]),
             pltpu.make_async_copy(pos_hbm, pos_ref, xsem.at[1])]
    for c in xload:
        c.start()
    for i in range(KCH):
        wq_copy(i).start()

    for ref, cond in ((wk_ref, colour < 8), (wv_ref, colour >= 8)):
        @pl.when((core == 1) & cond)
        def _():
            for i in range(KCH):
                wkv_copy(ref, i).start()

    mine = pl.multiple_of(core * 8, 8)
    theirs = pl.multiple_of(other * 8, 8)
    loc = [pltpu.make_async_copy(k_ref.at[pl.ds(mine, 8)], kbuf.at[:, core], ksem.at[0]),
           pltpu.make_async_copy(v_ref.at[pl.ds(mine, 8)], vbuf.at[:, core], ksem.at[1]),
           pltpu.make_async_copy(wo_ref, wob.at[core], ksem.at[2]),
           pltpu.make_async_copy(k_ref.at[pl.ds(theirs, 8)], khalf, ksem.at[3]),
           pltpu.make_async_copy(v_ref.at[pl.ds(theirs, 8)], vhalf, ksem.at[4])]

    bar = pltpu.get_barrier_semaphore()
    partner = chip * 2 + other
    for o in offsets():
        pl.semaphore_signal(bar, inc=1, device_id=dev(chip_at(o) * 2 + core), device_id_type=MESH)
    for o in [(0, 0, 0)] + colour_offsets():
        pl.semaphore_signal(bar, inc=1, device_id=dev(chip_at(o) * 2 + other), device_id_type=MESH)
    near = start_distance(chip) <= 1

    @pl.when(near)
    def _():
        for d in range(64):
            pl.semaphore_signal(bar, inc=1, device_id=dev(d * 2 + other), device_id_type=MESH)

    col = lax.broadcasted_iota(jnp.int32, (64, 1024), 1)
    row = lax.broadcasted_iota(jnp.int32, (64, 1024), 0)
    colidx[...] = jnp.where(col % 8 == row // 8, chip * 128 + col // 8, 1 << 30)

    for c in xload:
        c.wait()
    accq = jnp.zeros((16, 256), F32)
    for i in range(KCH):
        wq_copy(i).wait()
        if i == KCH // 2:
            for t in (3, 4, 0, 1):
                loc[t].start()
        accq = accq + jnp.dot(x_ref[:, i * rows:(i + 1) * rows], wqb[i * rows:(i + 1) * rows, :],
                              preferred_element_type=F32)
    for h in range(2):
        qsend[h] = accq[h * 8:h * 8 + 8].astype(BF16)
    loc[2].start()
    pl.semaphore_wait(bar, 79 + len(NEAR))

    def rcopy(src, dst, ss, rs, d):
        return pltpu.make_async_remote_copy(src_ref=src, dst_ref=dst, send_sem=ss, recv_sem=rs,
                                            device_id=dev(d), device_id_type=MESH)

    near_chips = [chip_at(o) for o in colour_offsets()]
    for ch in near_chips:
        for c2 in (core, other):
            rcopy(qsend.at[c2], qrecv.at[slot], q_send.at[0], q_recv.at[0], ch * 2 + c2).start()
    rcopy(qsend.at[other], qrecv.at[slot], q_send.at[0], q_recv.at[0], partner).start()
    loc[3].wait()
    loc[4].wait()
    dk = [rcopy(khalf.at[b], kbuf.at[b, core], d2d_send.at[b], d2d_recv.at[b], partner) for b in range(8)]
    dv = [rcopy(vhalf.at[b], vbuf.at[b, core], d2d_send.at[8 + b], d2d_recv.at[8 + b], partner) for b in range(8)]
    dw = rcopy(wo_ref, wob.at[core], d2d_send.at[16], d2d_recv.at[16], partner)
    dd = [c for pair in zip(dk, dv) for c in pair] + [dw]
    for c in dd:
        c.start()
    qrecv[slot] = qsend[core]

    @pl.when(core == 1)
    def _():
        acck = jnp.zeros((16, 128), F32)
        for i in range(KCH):
            wkv_copy(wk_ref, i).wait()
            acck = acck + jnp.dot(x_ref[:, i * rows:(i + 1) * rows], wkvb[i * rows:(i + 1) * rows, :],
                                  preferred_element_type=F32)
        for h in range(2):
            kvsend[h] = acck[h * 8:h * 8 + 8].astype(BF16)
        for ch in near_chips:
            for c2 in (core, other):
                rcopy(kvsend, kvrecv.at[colour], q_send.at[1], q_recv.at[1], ch * 2 + c2).start()
        rcopy(kvsend, kvrecv.at[colour], q_send.at[1], q_recv.at[1], partner).start()
        kvrecv[colour] = kvsend[...]

    def wait_all(ref, sem):
        pltpu.make_async_copy(ref, ref, sem).wait()

    wait_all(qrecv.at[pl.ds(0, 31)], q_recv.at[0])
    for s in range(32):
        q8 = qrecv[s].astype(F32)
        for j in range(2):
            qf[:, s * 2 + j, :] = q8[:, j * 128:(j + 1) * 128]

    @pl.when(core == 0)
    def _():
        wait_all(kvrecv.at[pl.ds(0, 16)], q_recv.at[1])

    @pl.when(core == 1)
    def _():
        wait_all(kvrecv.at[pl.ds(0, 15)], q_recv.at[1])

    for kv in range(2):
        for h in range(8):
            for half in range(2):
                kvf[kv, half, :, h, :] = kvrecv[kv * 8 + h, half].astype(F32)
    kvnew_ref[...] = kvf[...].astype(BF16)
    loc[0].wait()
    loc[1].wait()

    lane = lax.broadcasted_iota(jnp.int32, (64, 128), 1)
    stats = jnp.zeros((64, 128), F32)
    scale = 128 ** -0.5
    neg = -jnp.inf
    for b in range(8):
        pos = pos_ref[core * 8 + b]
        qb = qf[b]
        kn = jnp.broadcast_to(kvf[0, core, b][:, None, :], (8, 8, 128)).reshape(64, 128)
        vn = jnp.broadcast_to(kvf[1, core, b][:, None, :], (8, 8, 128)).reshape(64, 128)
        dk[b].wait_recv()
        s = lax.dot_general(qb.astype(BF16), kbuf[b].reshape(1024, 128), (((1,), (1,)), ((), ())),
                            preferred_element_type=F32) * scale
        s = jnp.where(colidx[...] < pos, s, neg)
        snew = jnp.sum(qb * kn, axis=1, keepdims=True) * scale
        here = jnp.full((64, 1), pos // 128, jnp.int32) == chip
        snew = jnp.where(here, snew, neg)
        m = jnp.maximum(jnp.max(s, axis=1, keepdims=True), snew)
        msafe = jnp.where(m == neg, 0.0, m)
        p = jnp.exp(s - msafe)
        pn = jnp.exp(snew - msafe)
        l = jnp.sum(p, axis=1, keepdims=True) + pn
        dv[b].wait_recv()
        o = jnp.dot(p.astype(BF16), vbuf[b].reshape(1024, 128), preferred_element_type=F32) + pn * vn
        osend[:, b, :] = o
        stats = jnp.where(lane == b, m, stats)
        stats = jnp.where(lane == 8 + b, l, stats)
    ssend[:, 0, :] = stats

    for o in offsets():
        d = chip_at(o)
        rcopy(osend.at[d], orecv.at[chip], o_send, o_recv, d * 2 + core).start()
        rcopy(ssend.at[d], srecv.at[chip], s_send, s_recv, d * 2 + core).start()
    orecv[chip] = osend[chip]
    srecv[chip] = ssend[chip]
    loc[2].wait()
    dw.wait_recv()
    wait_all(srecv.at[pl.ds(0, 63)], s_recv)
    st = jnp.concatenate([srecv[:, 0, :], jnp.zeros((64, 128), F32)], axis=0).T
    mt = st[0:8, 0:64]
    lt = st[8:16, 0:64]
    mx = jnp.max(mt, axis=1, keepdims=True)
    w = jnp.exp(mt - mx)
    tot = jnp.sum(w * lt, axis=1, keepdims=True)
    wait_all(orecv.at[pl.ds(0, 63)], o_recv)
    acc = jnp.zeros((8, 128), F32)
    for i in range(64):
        acc = acc + w[:, i:i + 1] * orecv[i]
    ob = (acc / tot).astype(BF16)

    pending = []
    for dz, dy in sorted([(a, b) for a in range(4) for b in range(4)], key=lambda o: -(RING[o[0]] + RING[o[1]])):
        r = ((cz + dz) % 4) * 4 + (cy + dy) % 4
        wj = wob[:, :, pl.ds(pl.multiple_of(r * 512, 512), 512)].reshape(128, 512)
        part = jnp.dot(ob, wj, preferred_element_type=F32)
        for jj in range(4):
            ysend[r * 4 + jj] = part[:, jj * 128:(jj + 1) * 128]
        for d in pending:
            rcopy(ysend.at[d], yrecv.at[chip], ys_send, ys_recv, d * 2 + core).start()
        pending = [chip_at((dz, dy, dx)) for dx in (2, 1, 3, 0) if (dz, dy, dx) != (0, 0, 0)]
    for d in pending:
        rcopy(ysend.at[d], yrecv.at[chip], ys_send, ys_recv, d * 2 + core).start()
    yrecv[chip] = ysend[chip]
    wait_all(yrecv.at[pl.ds(0, 63)], ys_recv)
    acc = yrecv[0]
    for i in range(1, 64):
        acc = acc + yrecv[i]
    yb[...] = acc.astype(BF16)

    for o in offsets():
        rcopy(yb, yg.at[core, chip], yg_send, yg_recv, chip_at(o) * 2 + core).start()
    for t in NEAR:
        rcopy(yb, yg.at[core, chip], pn_send, pn_recv, t * 2 + other).start()
    yg[core, chip] = yb[...]
    wait_all(yg.at[0, pl.ds(0, 63)], yg_recv)
    fwd = rcopy(yg.at[core], yg.at[core], pp_send, pp_recv, partner)

    @pl.when(near)
    def _():
        wait_all(yg.at[0], pn_recv)

    @pl.when(jnp.logical_not(near))
    def _():
        fwd.start()
        fwd.wait_recv()
        fwd.wait_send()

    out = pltpu.make_async_copy(yg, y_ref, ksem.at[0])
    out.start()

    wait_all(yg.at[0, pl.ds(0, 63)], yg_send)
    wait_all(yg.at[0, pl.ds(0, len(NEAR))], pn_send)
    wait_all(yrecv.at[pl.ds(0, 63)], ys_send)
    wait_all(orecv.at[pl.ds(0, 63)], o_send)
    wait_all(srecv.at[pl.ds(0, 63)], s_send)
    wait_all(qrecv.at[pl.ds(0, 31)], q_send.at[0])

    @pl.when(core == 1)
    def _():
        wait_all(kvrecv.at[pl.ds(0, 16)], q_send.at[1])
        wait_all(kvrecv.at[pl.ds(0, 15)], q_send.at[1])

    for c in dd:
        c.wait_send()
    out.wait()


EARLY = 3


def reads_and_writes(srcs, dsts, buf, isem, osem):
    rd = lambda t, i: pltpu.make_async_copy(srcs[t].at[pl.ds(i * 2, 2)], buf.at[t, pl.ds(i * 2, 2)], isem.at[t, i])
    wr = lambda t, i: pltpu.make_async_copy(buf.at[t, pl.ds(i * 2, 2)], dsts[t].at[pl.ds(i * 2, 2)], osem.at[t, i])
    return rd, wr


def copy_kernel(k_ref, v_ref, ko_ref, vo_ref, buf, isem, osem):
    chip = lax.axis_index("seq") // 2
    rd, wr = reads_and_writes((k_ref, v_ref), (ko_ref, vo_ref), buf, isem, osem)
    order = [(t, i) for i in range(8) for t in range(2)]

    @pl.when(start_distance(chip) <= EARLY)
    def _():
        for t, i in order:
            rd(t, i).start()
        for t, i in order:
            rd(t, i).wait()
            wr(t, i).start()
        for t, i in order:
            wr(t, i).wait()


def update_kernel(pos_ref, new_ref, y_ref, k_ref, v_ref, km_ref, vm_ref, yo_ref, ko_ref, vo_ref,
                  buf, ysem, isem, osem, rsem):
    me = lax.axis_index("seq")
    base = me * 64
    early = start_distance(me // 2) <= EARLY
    yout = pltpu.make_async_copy(y_ref, yo_ref, ysem)
    yout.start()
    dsts = (ko_ref, vo_ref)
    rd, wr = reads_and_writes((k_ref, v_ref), dsts, buf, isem, osem)
    order = [(t, i) for i in range(8) for t in range(2)]

    def inside(b):
        r = pos_ref[b] - base
        return r, (r >= 0) & (r < 64)

    @pl.when(early)
    def _():
        def row(t, b, r):
            return pltpu.make_async_copy(new_ref.at[t, b], dsts[t].at[b, r], rsem.at[t, b])

        for b in range(16):
            r, ok = inside(b)

            @pl.when(ok)
            def _():
                for t in range(2):
                    row(t, b, r).start()
        for b in range(16):
            r, ok = inside(b)

            @pl.when(ok)
            def _():
                for t in range(2):
                    row(t, b, r).wait()

    @pl.when(jnp.logical_not(early))
    def _():
        for t, i in order:
            rd(t, i).start()
        for t, i in order:
            rd(t, i).wait()
            for b in (2 * i, 2 * i + 1):
                r, ok = inside(b)

                @pl.when(ok)
                def _():
                    buf[t, b, r] = new_ref[t, b]
            wr(t, i).start()
        for t, i in order:
            wr(t, i).wait()

    yout.wait()


def solution(mesh):
    cache_spec = P('rep', 'seq', None, None)
    in_specs = (P('rep', None), P(), P(), P(), P('seq', None), cache_spec, cache_spec, P('rep'))
    out_specs = (P('rep', None), cache_spec, cache_spec)
    vmem, anyspace, smem = (pl.BlockSpec(memory_space=s) for s in (pltpu.VMEM, pl.ANY, pltpu.SMEM))
    dma = pltpu.SemaphoreType.DMA

    def local_step(x, wq, wk, wv, wo, k, v, pos):
        hbm = lambda *a: [pltpu.with_memory_space_constraint(t, pltpu.HBM) for t in a]
        cache = jax.ShapeDtypeStruct(k.shape, BF16)
        stage = [pltpu.VMEM((2, 16, 64, 8, 128), BF16), dma((2, 8)), dma((2, 8))]
        km, vm = pl.pallas_call(
            copy_kernel,
            name="copy_caches",
            out_shape=(cache, cache),
            in_specs=[anyspace] * 2,
            out_specs=(anyspace,) * 2,
            scratch_shapes=stage,
            compiler_params=pltpu.CompilerParams(vmem_limit_bytes=24 << 20),
        )(*hbm(k, v))
        x, km, vm = lax.optimization_barrier((x, km, vm))
        y, new = pl.pallas_call(
            main_kernel,
            name="decode",
            out_shape=(jax.ShapeDtypeStruct((2, 64, 8, 128), BF16),
                       jax.ShapeDtypeStruct((2, 2, 8, 8, 128), BF16)),
            in_specs=[anyspace] * 8,
            out_specs=(anyspace, vmem),
            scratch_shapes=[
                pltpu.SMEM((16,), jnp.int32), pltpu.VMEM((16, 8192), BF16),
                pltpu.VMEM((8, 512, 128), BF16), pltpu.VMEM((8, 512, 128), BF16),
                pltpu.VMEM((8192, 256), BF16), pltpu.VMEM((8192, 128), BF16),
                pltpu.VMEM((8, 2, 512, 128), BF16), pltpu.VMEM((8, 2, 512, 128), BF16),
                pltpu.VMEM((2, 64, 8192), BF16),
                pltpu.VMEM((2, 8, 256), BF16), pltpu.VMEM((32, 8, 256), BF16),
                pltpu.VMEM((2, 8, 128), BF16), pltpu.VMEM((16, 2, 8, 128), BF16),
                pltpu.VMEM((2, 2, 8, 8, 128), F32), pltpu.VMEM((8, 64, 128), F32),
                pltpu.VMEM((64, 1024), jnp.int32),
                pltpu.VMEM((64, 8, 128), F32), pltpu.VMEM((64, 8, 128), F32),
                pltpu.VMEM((64, 1, 128), F32), pltpu.VMEM((64, 1, 128), F32),
                pltpu.VMEM((64, 8, 128), F32), pltpu.VMEM((64, 8, 128), F32),
                pltpu.VMEM((8, 128), BF16), pltpu.VMEM((2, 64, 8, 128), BF16),
                dma((2,)), dma((2 * KCH,)), dma((5,)), dma((17,)), dma((17,)), dma((2,)), dma((2,)),
                dma, dma, dma, dma, dma, dma, dma, dma, dma, dma, dma, dma,
            ],
            compiler_params=pltpu.CompilerParams(collective_id=0, has_side_effects=True,
                                                 vmem_limit_bytes=DECODE_VMEM << 20),
        )(*hbm(pos, x, wq, wk, wv, wo, k.reshape(16, 512, 128), v.reshape(16, 512, 128)))
        yo, ko, vo = pl.pallas_call(
            update_kernel,
            name="update",
            out_shape=(jax.ShapeDtypeStruct(y.shape, BF16), cache, cache),
            in_specs=[smem, vmem, vmem] + [anyspace] * 4,
            out_specs=(anyspace,) * 3,
            scratch_shapes=[stage[0], dma, stage[1], stage[2], dma((2, 16))],
            input_output_aliases={5: 1, 6: 2},
            compiler_params=pltpu.CompilerParams(vmem_limit_bytes=24 << 20),
        )(pos, new.reshape(2, 16, 8, 128), y, *hbm(k, v, km, vm))
        return yo.transpose(0, 2, 1, 3).reshape(16, 8192), ko, vo

    return jax.shard_map(local_step, mesh=mesh, in_specs=in_specs, out_specs=out_specs, check_vma=False)
```

time: 49.4 us -> 48.7 us (0.986); the launches traced: 49.2 us -> 47.9 us
  local copies, waits for them, and re-layouts: 3.14 us -> 0.01 us
  Pallas kernels: 45.4 us -> 47.3 us
    pallas_call x0 -> x1, Pallas kernels: none -> 3.88 us  [local_step(): pl.pallas_call(copy_kernel, name='copy_caches', out_shape=(cache, cache),...]
    unnamed x11 -> x2, local copies, waits for them, and re-layouts: 3.14 us -> 0.01 us
    pallas_call x1, Pallas kernels: 3.14 us -> 1.83 us  [local_step(): pl.pallas_call(update_kernel, name='update', out_shape=(jax.ShapeDtypeStr...]
    pallas_call x1, Pallas kernels: 42.3 us -> 41.6 us  [local_step(): pl.pallas_call(main_kernel, name='decode', out_shape=(jax.ShapeDtypeStruc...]
where the time goes in v2:
time: 48.7 us; the launch traced here: 47.9 us
  Pallas kernels  47.3 us (97%)
  between operations  0.66 us (1%)
    pallas_call x1, Pallas kernels, local_step(): pl.pallas_call(main_kernel, name='decode', out_shape=(jax.ShapeDtypeStruc...  41.6 us
    pallas_call x1, Pallas kernels, local_step(): pl.pallas_call(copy_kernel, name='copy_caches', out_shape=(cache, cache),...  3.88 us
    pallas_call x1, Pallas kernels, local_step(): pl.pallas_call(update_kernel, name='update', out_shape=(jax.ShapeDtypeStr...  1.83 us

profile of v2, /device:TPU:1, one launch (start us, length us, event | category | flops | bytes accessed | tf_op | source)
XLA Modules:
  0.0 47.9 jit_solution(16519812332907366819)
XLA Ops:
  0.6 3.9 %copy_caches.1 = (bf16[16,64,8,128]{3,2,1,0:T(8,128)(2,1)}, bf16[16,64,8,128]{3,2,1,0:T(8,128)(2,1)}) custom-call(bf16[16,64,8,128]{3,2,1,0:T(8,128)(2,1)} %k_ref.3, bf16[16,64,8,128]{3,2,1,0:T(8,128)(2,1)} %v_ref.3), custom_call_target="tpu_custom_call" | custom-call | tf_op jit(solution)/shard_map/copy_caches/pallas_call | solution.py:385
  4.5 0.0 copy-start
  4.5 41.6 %decode.1 = (bf16[2,64,8,128]{3,2,1,0:T(8,128)(2,1)S(1)}, bf16[2,2,8,8,128]{4,3,2,1,0:T(8,128)(2,1)S(1)}) custom-call(s32[16]{0:T(128)} %pos_ref.1, bf16[16,8192]{1,0:T(8,128)(2,1)} %x_hbm, bf16[8192,8192]{1,0:T(8,128)(2,1)} %wq_ref.1, bf16[8192,1024]{1,0:T(8,128)(2,1)} %wk_ref.1, bf16[8192,1024]{1,0:T(8,128)(2,1)} %wv_ref.1, bf16[64,8192]{1,0:T(8,128)(2,1)} %wo_ref.1, ...), custom_call_target="tpu_custom_call" | custom-call | tf_op jit(solution)/shard_map/decode/pallas_call | solution.py:395
  46.1 0.0 copy-done
  46.1 1.8 %update.1 = (bf16[2,64,8,128]{3,2,1,0:T(8,128)(2,1)}, bf16[16,64,8,128]{3,2,1,0:T(8,128)(2,1)}, bf16[16,64,8,128]{3,2,1,0:T(8,128)(2,1)}) custom-call(s32[16]{0:T(128)S(1)} %copy-done, bf16[2,16,8,128]{3,2,1,0:T(8,128)(2,1)S(1)} %bitcast.6, bf16[2,64,8,128]{3,2,1,0:T(8,128)(2,1)S(1)} %get-tuple-element.17.y_ref, ...), custom_call_target="tpu_custom_call", output_to_operand_aliasing={{1}: (5, {}), {2}: (6, {})} | custom-call | tf_op jit(solution)/shard_map/update/pallas_call | solution.py:422
Async XLA Ops:
  4.5 41.6 %copy-start = (s32[16]{0:T(128)S(1)}, s32[16]{0:T(128)}, u32[]{:S(2)}) copy-start(s32[16]{0:T(128)} %pos_ref.1) | copy-start | bytes 196

commit v3 on v2

v3 whole, which is shorter than its diff:
```python
import functools
import jax
import jax.numpy as jnp
from jax import lax
from jax.experimental import pallas as pl
from jax.experimental.pallas import tpu as pltpu
from jax.sharding import PartitionSpec as P

BF16 = jnp.bfloat16
F32 = jnp.float32
MESH = pl.DeviceIdType.MESH
DECODE_VMEM = 40
KCH = 8
RING = (0, 1, 2, 1)


def offsets():
    offs = [(dz, dy, dx) for dz in range(4) for dy in range(4) for dx in range(4)][1:]
    return sorted(offs, key=lambda o: -(RING[o[0]] + RING[o[1]] + RING[o[2]]))


def hops(o):
    return RING[o[0]] + RING[o[1]] + RING[o[2]]


def colour_offsets():
    best = {}
    for o in sorted(offsets(), key=lambda o: (hops(o), o)):
        d = ((o[2] + o[0]) % 4, (o[1] + o[0]) % 4)
        neg = ((-d[0]) % 4, (-d[1]) % 4)
        if d == (0, 0) or d in best or (d == neg and any(c % 2 for c in o)):
            continue
        best[d] = o
        best[neg] = tuple(-c % 4 for c in o)
    return sorted(best.values(), key=lambda o: -hops(o))


NEAR = [0, 1, 4]


def main_kernel(pos_hbm, x_hbm, wq_ref, wk_ref, wv_ref, wo_ref, k_ref, v_ref,
                y_ref, kvnew_ref, km_ref, vm_ref,
                pos_ref, x_ref, wqb, wkvb, kbuf, vbuf, wob, qsend, qrecv, kvsend, kvrecv, kvf, qf, colidx,
                opart, opeer, speer, oown, osend, orecv, ssend, srecv, ysend, yrecv, yb, yg,
                xsem, wsem, ksem, dw_send, dw_recv, d2d_send, d2d_recv, q_send, q_recv, o_send, o_recv,
                s_send, s_recv, ys_send, ys_recv, yg_send, yg_recv, pp_send, pp_recv, pn_send, pn_recv):
    me = lax.axis_index("seq")
    chip, core = me // 2, me % 2
    cx, cy, cz = chip % 4, (chip // 4) % 4, chip // 16
    other = 1 - core
    colour = ((cx + cz) % 4) * 4 + (cy + cz) % 4
    slot = colour * 2 + core

    def dev(d):
        return {"seq": d}

    def chip_at(o):
        return ((cz + o[0]) % 4) * 16 + ((cy + o[1]) % 4) * 4 + (cx + o[2]) % 4

    rows = 8192 // KCH
    qcol = pl.multiple_of(slot * 256, 256)
    kcol = pl.multiple_of((colour % 8) * 128, 128)

    def wq_copy(i):
        return pltpu.make_async_copy(wq_ref.at[pl.ds(i * rows, rows), pl.ds(qcol, 256)],
                                     wqb.at[pl.ds(i * rows, rows)], wsem.at[i])

    def wkv_copy(ref, i):
        return pltpu.make_async_copy(ref.at[pl.ds(i * rows, rows), pl.ds(kcol, 128)],
                                     wkvb.at[pl.ds(i * rows, rows)], wsem.at[KCH + i])

    xload = [pltpu.make_async_copy(x_hbm, x_ref, xsem.at[0]),
             pltpu.make_async_copy(pos_hbm, pos_ref, xsem.at[1])]
    for c in xload:
        c.start()
    for i in range(KCH):
        wq_copy(i).start()

    for ref, cond in ((wk_ref, colour < 8), (wv_ref, colour >= 8)):
        @pl.when((core == 1) & cond)
        def _():
            for i in range(KCH):
                wkv_copy(ref, i).start()

    loc = [pltpu.make_async_copy(k_ref, kbuf, ksem.at[0]),
           pltpu.make_async_copy(v_ref, vbuf, ksem.at[1]),
           pltpu.make_async_copy(wo_ref, wob.at[core], ksem.at[2]),
           pltpu.make_async_copy(k_ref, km_ref, ksem.at[3]),
           pltpu.make_async_copy(v_ref, vm_ref, ksem.at[4])]

    bar = pltpu.get_barrier_semaphore()
    partner = chip * 2 + other
    for o in offsets():
        pl.semaphore_signal(bar, inc=1, device_id=dev(chip_at(o) * 2 + core), device_id_type=MESH)
    for o in [(0, 0, 0)] + colour_offsets():
        pl.semaphore_signal(bar, inc=1, device_id=dev(chip_at(o) * 2 + other), device_id_type=MESH)
    near = functools.reduce(jnp.logical_or, [chip == c for c in NEAR])

    @pl.when(near)
    def _():
        for d in range(64):
            pl.semaphore_signal(bar, inc=1, device_id=dev(d * 2 + other), device_id_type=MESH)

    col = lax.broadcasted_iota(jnp.int32, (64, 512), 1)
    row = lax.broadcasted_iota(jnp.int32, (64, 512), 0)
    colidx[...] = jnp.where(col % 8 == row // 8, me * 64 + col // 8, 1 << 30)

    for c in xload:
        c.wait()
    accq = jnp.zeros((16, 256), F32)
    for i in range(KCH):
        wq_copy(i).wait()
        if i == KCH // 2:
            loc[0].start()
            loc[1].start()
        accq = accq + jnp.dot(x_ref[:, i * rows:(i + 1) * rows], wqb[i * rows:(i + 1) * rows, :],
                              preferred_element_type=F32)
    qsend[...] = accq.astype(BF16)
    loc[2].start()
    pl.semaphore_wait(bar, 79 + len(NEAR))

    def rcopy(src, dst, ss, rs, d):
        return pltpu.make_async_remote_copy(src_ref=src, dst_ref=dst, send_sem=ss, recv_sem=rs,
                                            device_id=dev(d), device_id_type=MESH)

    near_chips = [chip_at(o) for o in colour_offsets()]
    for ch in near_chips:
        for c2 in (core, other):
            rcopy(qsend, qrecv.at[slot], q_send.at[0], q_recv.at[0], ch * 2 + c2).start()
    rcopy(qsend, qrecv.at[slot], q_send.at[0], q_recv.at[0], partner).start()
    qrecv[slot] = qsend[...]

    @pl.when(core == 1)
    def _():
        acck = jnp.zeros((16, 128), F32)
        for i in range(KCH):
            wkv_copy(wk_ref, i).wait()
            acck = acck + jnp.dot(x_ref[:, i * rows:(i + 1) * rows], wkvb[i * rows:(i + 1) * rows, :],
                                  preferred_element_type=F32)
        for h in range(2):
            kvsend[h] = acck[h * 8:h * 8 + 8].astype(BF16)
        for ch in near_chips:
            for c2 in (core, other):
                rcopy(kvsend, kvrecv.at[colour], q_send.at[1], q_recv.at[1], ch * 2 + c2).start()
        rcopy(kvsend, kvrecv.at[colour], q_send.at[1], q_recv.at[1], partner).start()
        kvrecv[colour] = kvsend[...]

    def wait_all(ref, sem):
        pltpu.make_async_copy(ref, ref, sem).wait()

    wait_all(qrecv.at[pl.ds(0, 31)], q_recv.at[0])
    dw = rcopy(wo_ref, wob.at[core], dw_send, dw_recv, partner)
    dw.start()
    for s in range(32):
        q8 = qrecv[s].astype(F32)
        for j in range(2):
            qf[:, s * 2 + j, :] = q8[:, j * 128:(j + 1) * 128]

    @pl.when(core == 0)
    def _():
        wait_all(kvrecv.at[pl.ds(0, 16)], q_recv.at[1])

    @pl.when(core == 1)
    def _():
        wait_all(kvrecv.at[pl.ds(0, 15)], q_recv.at[1])

    for kv in range(2):
        for h in range(8):
            for half in range(2):
                kvf[kv, half, :, h, :] = kvrecv[kv * 8 + h, half].astype(F32)
    kvnew_ref[...] = kvf[...].astype(BF16)
    loc[0].wait()
    loc[1].wait()

    lane = lax.broadcasted_iota(jnp.int32, (64, 128), 1)
    scale = 128 ** -0.5
    neg = -jnp.inf

    def attend(half, dst):
        stats = jnp.zeros((64, 128), F32)
        for i in range(8):
            b = half * 8 + i
            pos = pos_ref[b]
            qb = qf[b]
            kn = jnp.broadcast_to(kvf[0, half, i][:, None, :], (8, 8, 128)).reshape(64, 128)
            vn = jnp.broadcast_to(kvf[1, half, i][:, None, :], (8, 8, 128)).reshape(64, 128)
            s = lax.dot_general(qb.astype(BF16), kbuf[b], (((1,), (1,)), ((), ())),
                                preferred_element_type=F32) * scale
            s = jnp.where(colidx[...] < pos, s, neg)
            snew = jnp.sum(qb * kn, axis=1, keepdims=True) * scale
            here = jnp.full((64, 1), pos // 64, jnp.int32) == me
            snew = jnp.where(here, snew, neg)
            m = jnp.maximum(jnp.max(s, axis=1, keepdims=True), snew)
            msafe = jnp.where(m == neg, 0.0, m)
            p = jnp.exp(s - msafe)
            pn = jnp.exp(snew - msafe)
            l = jnp.sum(p, axis=1, keepdims=True) + pn
            dst[i] = jnp.dot(p.astype(BF16), vbuf[b], preferred_element_type=F32) + pn * vn
            stats = jnp.where(lane == i, m, stats)
            stats = jnp.where(lane == 8 + i, l, stats)
        return stats

    ssend[:, 0, :] = attend(other, opart)
    do = [rcopy(opart, opeer, d2d_send.at[0], d2d_recv.at[0], partner),
          rcopy(ssend, speer, d2d_send.at[1], d2d_recv.at[1], partner)]
    for c in do:
        c.start()
    st1 = attend(core, oown)
    do[1].wait()
    st2 = speer[:, 0, :]
    do[0].wait()
    stats = jnp.zeros((64, 128), F32)
    for i in range(8):
        m1, m2 = st1[:, i:i + 1], st2[:, i:i + 1]
        l1, l2 = st1[:, 8 + i:9 + i], st2[:, 8 + i:9 + i]
        m = jnp.maximum(m1, m2)
        msafe = jnp.where(m == neg, 0.0, m)
        w1, w2 = jnp.exp(m1 - msafe), jnp.exp(m2 - msafe)
        osend[:, i, :] = w1 * oown[i] + w2 * opeer[i]
        stats = jnp.where(lane == i, m, stats)
        stats = jnp.where(lane == 8 + i, w1 * l1 + w2 * l2, stats)
    ssend[:, 0, :] = stats

    for o in offsets():
        d = chip_at(o)
        rcopy(osend.at[d], orecv.at[chip], o_send, o_recv, d * 2 + core).start()
        rcopy(ssend.at[d], srecv.at[chip], s_send, s_recv, d * 2 + core).start()
    loc[3].start()
    loc[4].start()
    orecv[chip] = osend[chip]
    srecv[chip] = ssend[chip]
    loc[2].wait()
    dw.wait_recv()
    wait_all(srecv.at[pl.ds(0, 63)], s_recv)
    st = jnp.concatenate([srecv[:, 0, :], jnp.zeros((64, 128), F32)], axis=0).T
    mt = st[0:8, 0:64]
    lt = st[8:16, 0:64]
    mx = jnp.max(mt, axis=1, keepdims=True)
    w = jnp.exp(mt - mx)
    tot = jnp.sum(w * lt, axis=1, keepdims=True)
    wait_all(orecv.at[pl.ds(0, 63)], o_recv)
    acc = jnp.zeros((8, 128), F32)
    for i in range(64):
        acc = acc + w[:, i:i + 1] * orecv[i]
    ob = (acc / tot).astype(BF16)

    pending = []
    for dz, dy in sorted([(a, b) for a in range(4) for b in range(4)], key=lambda o: -(RING[o[0]] + RING[o[1]])):
        r = ((cz + dz) % 4) * 4 + (cy + dy) % 4
        wj = wob[:, :, pl.ds(pl.multiple_of(r * 512, 512), 512)].reshape(128, 512)
        part = jnp.dot(ob, wj, preferred_element_type=F32)
        for jj in range(4):
            ysend[r * 4 + jj] = part[:, jj * 128:(jj + 1) * 128]
        for d in pending:
            rcopy(ysend.at[d], yrecv.at[chip], ys_send, ys_recv, d * 2 + core).start()
        pending = [chip_at((dz, dy, dx)) for dx in (2, 1, 3, 0) if (dz, dy, dx) != (0, 0, 0)]
    for d in pending:
        rcopy(ysend.at[d], yrecv.at[chip], ys_send, ys_recv, d * 2 + core).start()
    yrecv[chip] = ysend[chip]
    wait_all(yrecv.at[pl.ds(0, 63)], ys_recv)
    acc = yrecv[0]
    for i in range(1, 64):
        acc = acc + yrecv[i]
    yb[...] = acc.astype(BF16)

    for o in offsets():
        rcopy(yb, yg.at[core, chip], yg_send, yg_recv, chip_at(o) * 2 + core).start()
    for t in NEAR:
        rcopy(yb, yg.at[core, chip], pn_send, pn_recv, t * 2 + other).start()
    yg[core, chip] = yb[...]
    wait_all(yg.at[0, pl.ds(0, 63)], yg_recv)
    fwd = rcopy(yg.at[core], yg.at[core], pp_send, pp_recv, partner)

    @pl.when(near)
    def _():
        wait_all(yg.at[0], pn_recv)

    @pl.when(jnp.logical_not(near))
    def _():
        fwd.start()
        fwd.wait_recv()
        fwd.wait_send()

    out = pltpu.make_async_copy(yg, y_ref, ksem.at[0])
    out.start()

    wait_all(yg.at[0, pl.ds(0, 63)], yg_send)
    wait_all(yg.at[0, pl.ds(0, len(NEAR))], pn_send)
    wait_all(yrecv.at[pl.ds(0, 63)], ys_send)
    wait_all(orecv.at[pl.ds(0, 63)], o_send)
    wait_all(srecv.at[pl.ds(0, 63)], s_send)
    wait_all(qrecv.at[pl.ds(0, 31)], q_send.at[0])

    @pl.when(core == 1)
    def _():
        wait_all(kvrecv.at[pl.ds(0, 16)], q_send.at[1])
        wait_all(kvrecv.at[pl.ds(0, 15)], q_send.at[1])

    dw.wait_send()
    loc[3].wait()
    loc[4].wait()
    out.wait()


def update_kernel(pos_ref, new_ref, y_ref, k_ref, v_ref, yo_ref, ko_ref, vo_ref, patch, ysem, sem):
    base = lax.axis_index("seq") * 64
    yout = pltpu.make_async_copy(y_ref, yo_ref, ysem)
    yout.start()
    pairs = ((k_ref, ko_ref), (v_ref, vo_ref))
    for b in range(16):
        r = pos_ref[b] - base
        inside = (r >= 0) & (r < 64)
        for t, (src, dst) in enumerate(pairs):
            @pl.when(jnp.logical_not(inside))
            def _():
                pltpu.make_async_copy(src.at[b], dst.at[b], sem.at[t, b]).start()

            @pl.when(inside)
            def _():
                patch[t, b] = src[b]
                patch[t, b, r] = new_ref[t, b]
                pltpu.make_async_copy(patch.at[t, b], dst.at[b], sem.at[t, b]).start()
    for b in range(16):
        for t, (src, dst) in enumerate(pairs):
            pltpu.make_async_copy(patch.at[t, b], dst.at[b], sem.at[t, b]).wait()
    yout.wait()


def solution(mesh):
    cache_spec = P('rep', 'seq', None, None)
    in_specs = (P('rep', None), P(), P(), P(), P('seq', None), cache_spec, cache_spec, P('rep'))
    out_specs = (P('rep', None), cache_spec, cache_spec)
    vmem, anyspace, smem = (pl.BlockSpec(memory_space=s) for s in (pltpu.VMEM, pl.ANY, pltpu.SMEM))
    dma = pltpu.SemaphoreType.DMA

    def local_step(x, wq, wk, wv, wo, k, v, pos):
        hbm = lambda *a: [pltpu.with_memory_space_constraint(t, pltpu.HBM) for t in a]
        half = jax.ShapeDtypeStruct((16, 512, 128), BF16)
        y, new, km, vm = pl.pallas_call(
            main_kernel,
            name="decode",
            out_shape=(jax.ShapeDtypeStruct((2, 64, 8, 128), BF16),
                       jax.ShapeDtypeStruct((2, 2, 8, 8, 128), BF16), half, half),
            in_specs=[anyspace] * 8,
            out_specs=(anyspace, vmem, anyspace, anyspace),
            scratch_shapes=[
                pltpu.SMEM((16,), jnp.int32), pltpu.VMEM((16, 8192), BF16),
                pltpu.VMEM((8192, 256), BF16), pltpu.VMEM((8192, 128), BF16),
                pltpu.VMEM((16, 512, 128), BF16), pltpu.VMEM((16, 512, 128), BF16),
                pltpu.VMEM((2, 64, 8192), BF16),
                pltpu.VMEM((16, 256), BF16), pltpu.VMEM((32, 16, 256), BF16),
                pltpu.VMEM((2, 8, 128), BF16), pltpu.VMEM((16, 2, 8, 128), BF16),
                pltpu.VMEM((2, 2, 8, 8, 128), F32), pltpu.VMEM((16, 64, 128), F32),
                pltpu.VMEM((64, 512), jnp.int32),
                pltpu.VMEM((8, 64, 128), F32), pltpu.VMEM((8, 64, 128), F32),
                pltpu.VMEM((64, 1, 128), F32), pltpu.VMEM((8, 64, 128), F32),
                pltpu.VMEM((64, 8, 128), F32), pltpu.VMEM((64, 8, 128), F32),
                pltpu.VMEM((64, 1, 128), F32), pltpu.VMEM((64, 1, 128), F32),
                pltpu.VMEM((64, 8, 128), F32), pltpu.VMEM((64, 8, 128), F32),
                pltpu.VMEM((8, 128), BF16), pltpu.VMEM((2, 64, 8, 128), BF16),
                dma((2,)), dma((2 * KCH,)), dma((5,)), dma, dma, dma((2,)), dma((2,)), dma((2,)), dma((2,)),
                dma, dma, dma, dma, dma, dma, dma, dma, dma, dma, dma, dma,
            ],
            compiler_params=pltpu.CompilerParams(collective_id=0, has_side_effects=True,
                                                 vmem_limit_bytes=DECODE_VMEM << 20),
        )(*hbm(pos, x, wq, wk, wv, wo, k.reshape(16, 512, 128), v.reshape(16, 512, 128)))
        yo, ko, vo = pl.pallas_call(
            update_kernel,
            name="update",
            out_shape=(jax.ShapeDtypeStruct(y.shape, BF16),) + (jax.ShapeDtypeStruct(k.shape, BF16),) * 2,
            in_specs=[smem, vmem, vmem, vmem, vmem],
            out_specs=(anyspace,) * 3,
            scratch_shapes=[pltpu.VMEM((2, 16, 64, 8, 128), BF16), dma, dma((2, 16))],
            compiler_params=pltpu.CompilerParams(vmem_limit_bytes=24 << 20),
        )(pos, new.reshape(2, 16, 8, 128), y, km.reshape(k.shape), vm.reshape(k.shape))
        return yo.transpose(0, 2, 1, 3).reshape(16, 8192), ko, vo

    return jax.shard_map(local_step, mesh=mesh, in_specs=in_specs, out_specs=out_specs, check_vma=False)
```

time: 48.7 us -> 45.3 us (0.930); the launches traced: 47.9 us -> 45.1 us
  Pallas kernels: 47.3 us -> 44.5 us
    pallas_call x1 -> x0, Pallas kernels: 3.88 us -> none  [local_step(): pl.pallas_call(copy_kernel, name='copy_caches', out_shape=(cache, cache),...]
    pallas_call x1, Pallas kernels: 1.83 us -> 2.9 us  [local_step(): pl.pallas_call(update_kernel, name='update', out_shape=(jax.ShapeDtypeStr...]
where the time goes in v3:
time: 45.3 us; the launch traced here: 45.1 us
  Pallas kernels  44.5 us (98%)
  between operations  0.66 us (1%)
    pallas_call x1, Pallas kernels, local_step(): pl.pallas_call(main_kernel, name='decode', out_shape=(jax.ShapeDtypeStruc...  41.6 us
    pallas_call x1, Pallas kernels, local_step(): pl.pallas_call(update_kernel, name='update', out_shape=(jax.ShapeDtypeStr...  2.9 us

profile of v3, /device:TPU:1, one launch (start us, length us, event | category | flops | bytes accessed | tf_op | source)
XLA Modules:
  0.0 45.1 jit_solution(1229413824300099025)
XLA Ops:
  0.6 0.0 copy-start
  0.6 41.6 %decode.1 = (bf16[2,64,8,128]{3,2,1,0:T(8,128)(2,1)S(1)}, bf16[2,2,8,8,128]{4,3,2,1,0:T(8,128)(2,1)S(1)}, bf16[16,512,128]{2,1,0:T(8,128)(2,1)S(1)}, bf16[16,512,128]{2,1,0:T(8,128)(2,1)S(1)}) custom-call(s32[16]{0:T(128)} %pos_ref.1, bf16[16,8192]{1,0:T(8,128)(2,1)} %x_hbm.1, bf16[8192,8192]{1,0:T(8,128)(2,1)} %wq_ref.1, bf16[8192,1024]{1,0:T(8,128)(2,1)} %wk_ref.1, ...), custom_call_target="tpu_custom_call" | custom-call | tf_op jit(solution)/shard_map/decode/pallas_call | solution.py:339
  42.2 0.0 copy-done
  42.2 2.9 %update.1 = (bf16[2,64,8,128]{3,2,1,0:T(8,128)(2,1)}, bf16[16,64,8,128]{3,2,1,0:T(8,128)(2,1)}, bf16[16,64,8,128]{3,2,1,0:T(8,128)(2,1)}) custom-call(s32[16]{0:T(128)S(1)} %copy-done, bf16[2,16,8,128]{3,2,1,0:T(8,128)(2,1)S(1)} %bitcast.10, bf16[2,64,8,128]{3,2,1,0:T(8,128)(2,1)S(1)} %get-tuple-element.11.y_ref, bf16[16,64,8,128]{3,2,1,0:T(8,128)(2,1)S(1)} %bitcast.8, ...), custom_call_target="tpu_custom_call" | custom-call | tf_op jit(solution)/shard_map/update/pallas_call | solution.py:367
Async XLA Ops:
  0.6 41.6 %copy-start = (s32[16]{0:T(128)S(1)}, s32[16]{0:T(128)}, u32[]{:S(2)}) copy-start(s32[16]{0:T(128)} %pos_ref.1) | copy-start | bytes 196

commit v4 on v3

--- a/solution.py
+++ b/solution.py
@@ -42,7 +42,7 @@
                 y_ref, kvnew_ref, km_ref, vm_ref,
                 pos_ref, x_ref, wqb, wkvb, kbuf, vbuf, wob, qsend, qrecv, kvsend, kvrecv, kvf, qf, colidx,
                 opart, opeer, speer, oown, osend, orecv, ssend, srecv, ysend, yrecv, yb, yg,
-                xsem, wsem, ksem, dw_send, dw_recv, d2d_send, d2d_recv, q_send, q_recv, o_send, o_recv,
+                ring_sem, xsem, wsem, ksem, dw_send, dw_recv, d2d_send, d2d_recv, q_send, q_recv, o_send, o_recv,
                 s_send, s_recv, ys_send, ys_recv, yg_send, yg_recv, pp_send, pp_recv, pn_send, pn_recv):
     me = lax.axis_index("seq")
     chip, core = me // 2, me % 2
@@ -90,16 +90,21 @@
 
     bar = pltpu.get_barrier_semaphore()
     partner = chip * 2 + other
-    for o in offsets():
-        pl.semaphore_signal(bar, inc=1, device_id=dev(chip_at(o) * 2 + core), device_id_type=MESH)
-    for o in [(0, 0, 0)] + colour_offsets():
-        pl.semaphore_signal(bar, inc=1, device_id=dev(chip_at(o) * 2 + other), device_id_type=MESH)
+    near_chips = [chip_at(o) for o in colour_offsets()]
+    for ch in near_chips:
+        for c2 in (core, other):
+            pl.semaphore_signal(bar, inc=1, device_id=dev(ch * 2 + c2), device_id_type=MESH)
+    pl.semaphore_signal(bar, inc=1, device_id=dev(partner), device_id_type=MESH)
     near = functools.reduce(jnp.logical_or, [chip == c for c in NEAR])
 
-    @pl.when(near)
-    def _():
-        for d in range(64):
-            pl.semaphore_signal(bar, inc=1, device_id=dev(d * 2 + other), device_id_type=MESH)
+    def greet(axis):
+        for t in (2, 1, 3):
+            o = [0, 0, 0]
+            o[axis] = t
+            pl.semaphore_signal(ring_sem.at[axis], inc=1, device_id=dev(chip_at(o) * 2 + core), device_id_type=MESH)
+
+    def greeted(axis):
+        pl.semaphore_wait(ring_sem.at[axis], 3)
 
     col = lax.broadcasted_iota(jnp.int32, (64, 512), 1)
     row = lax.broadcasted_iota(jnp.int32, (64, 512), 0)
@@ -117,13 +122,13 @@
                               preferred_element_type=F32)
     qsend[...] = accq.astype(BF16)
     loc[2].start()
-    pl.semaphore_wait(bar, 79 + len(NEAR))
+    pl.semaphore_wait(bar, 31)
+    greet(2)
 
     def rcopy(src, dst, ss, rs, d):
         return pltpu.make_async_remote_copy(src_ref=src, dst_ref=dst, send_sem=ss, recv_sem=rs,
                                             device_id=dev(d), device_id_type=MESH)
 
-    near_chips = [chip_at(o) for o in colour_offsets()]
     for ch in near_chips:
         for c2 in (core, other):
             rcopy(qsend, qrecv.at[slot], q_send.at[0], q_recv.at[0], ch * 2 + c2).start()
@@ -148,6 +153,10 @@
     def wait_all(ref, sem):
         pltpu.make_async_copy(ref, ref, sem).wait()
 
+    greeted(2)
+    greet(1)
+    greeted(1)
+    greet(0)
     wait_all(qrecv.at[pl.ds(0, 31)], q_recv.at[0])
     dw = rcopy(wo_ref, wob.at[core], dw_send, dw_recv, partner)
     dw.start()
@@ -155,20 +164,6 @@
         q8 = qrecv[s].astype(F32)
         for j in range(2):
             qf[:, s * 2 + j, :] = q8[:, j * 128:(j + 1) * 128]
-
-    @pl.when(core == 0)
-    def _():
-        wait_all(kvrecv.at[pl.ds(0, 16)], q_recv.at[1])
-
-    @pl.when(core == 1)
-    def _():
-        wait_all(kvrecv.at[pl.ds(0, 15)], q_recv.at[1])
-
-    for kv in range(2):
-        for h in range(8):
-            for half in range(2):
-                kvf[kv, half, :, h, :] = kvrecv[kv * 8 + h, half].astype(F32)
-    kvnew_ref[...] = kvf[...].astype(BF16)
     loc[0].wait()
     loc[1].wait()
 
@@ -182,20 +177,13 @@
             b = half * 8 + i
             pos = pos_ref[b]
             qb = qf[b]
-            kn = jnp.broadcast_to(kvf[0, half, i][:, None, :], (8, 8, 128)).reshape(64, 128)
-            vn = jnp.broadcast_to(kvf[1, half, i][:, None, :], (8, 8, 128)).reshape(64, 128)
             s = lax.dot_general(qb.astype(BF16), kbuf[b], (((1,), (1,)), ((), ())),
                                 preferred_element_type=F32) * scale
             s = jnp.where(colidx[...] < pos, s, neg)
-            snew = jnp.sum(qb * kn, axis=1, keepdims=True) * scale
-            here = jnp.full((64, 1), pos // 64, jnp.int32) == me
-            snew = jnp.where(here, snew, neg)
-            m = jnp.maximum(jnp.max(s, axis=1, keepdims=True), snew)
-            msafe = jnp.where(m == neg, 0.0, m)
-            p = jnp.exp(s - msafe)
-            pn = jnp.exp(snew - msafe)
-            l = jnp.sum(p, axis=1, keepdims=True) + pn
-            dst[i] = jnp.dot(p.astype(BF16), vbuf[b], preferred_element_type=F32) + pn * vn
+            m = jnp.max(s, axis=1, keepdims=True)
+            p = jnp.exp(s - jnp.where(m == neg, 0.0, m))
+            l = jnp.sum(p, axis=1, keepdims=True)
+            dst[i] = jnp.dot(p.astype(BF16), vbuf[b], preferred_element_type=F32)
             stats = jnp.where(lane == i, m, stats)
             stats = jnp.where(lane == 8 + i, l, stats)
         return stats
@@ -206,6 +194,21 @@
     for c in do:
         c.start()
     st1 = attend(core, oown)
+
+    @pl.when(core == 0)
+    def _():
+        wait_all(kvrecv.at[pl.ds(0, 16)], q_recv.at[1])
+
+    @pl.when(core == 1)
+    def _():
+        wait_all(kvrecv.at[pl.ds(0, 15)], q_recv.at[1])
+
+    for kv in range(2):
+        for h in range(8):
+            for half in range(2):
+                kvf[kv, half, :, h, :] = kvrecv[kv * 8 + h, half].astype(F32)
+    kvnew_ref[...] = kvf[...].astype(BF16)
+
     do[1].wait()
     st2 = speer[:, 0, :]
     do[0].wait()
@@ -213,13 +216,20 @@
     for i in range(8):
         m1, m2 = st1[:, i:i + 1], st2[:, i:i + 1]
         l1, l2 = st1[:, 8 + i:9 + i], st2[:, 8 + i:9 + i]
-        m = jnp.maximum(m1, m2)
+        kn = jnp.broadcast_to(kvf[0, core, i][:, None, :], (8, 8, 128)).reshape(64, 128)
+        vn = jnp.broadcast_to(kvf[1, core, i][:, None, :], (8, 8, 128)).reshape(64, 128)
+        snew = jnp.sum(qf[core * 8 + i] * kn, axis=1, keepdims=True) * scale
+        here = jnp.full((64, 1), pos_ref[core * 8 + i] // 128, jnp.int32) == chip
+        snew = jnp.where(here, snew, neg)
+        m = jnp.maximum(jnp.maximum(m1, m2), snew)
         msafe = jnp.where(m == neg, 0.0, m)
-        w1, w2 = jnp.exp(m1 - msafe), jnp.exp(m2 - msafe)
-        osend[:, i, :] = w1 * oown[i] + w2 * opeer[i]
+        w1, w2, w3 = jnp.exp(m1 - msafe), jnp.exp(m2 - msafe), jnp.exp(snew - msafe)
+        osend[:, i, :] = w1 * oown[i] + w2 * opeer[i] + w3 * vn
         stats = jnp.where(lane == i, m, stats)
-        stats = jnp.where(lane == 8 + i, w1 * l1 + w2 * l2, stats)
+        stats = jnp.where(lane == 8 + i, w1 * l1 + w2 * l2 + w3, stats)
     ssend[:, 0, :] = stats
+
+    greeted(0)
 
     for o in offsets():
         d = chip_at(o)
@@ -358,7 +368,7 @@
                 pltpu.VMEM((64, 1, 128), F32), pltpu.VMEM((64, 1, 128), F32),
                 pltpu.VMEM((64, 8, 128), F32), pltpu.VMEM((64, 8, 128), F32),
                 pltpu.VMEM((8, 128), BF16), pltpu.VMEM((2, 64, 8, 128), BF16),
-                dma((2,)), dma((2 * KCH,)), dma((5,)), dma, dma, dma((2,)), dma((2,)), dma((2,)), dma((2,)),
+                pltpu.SemaphoreType.REGULAR((3,)), dma((2,)), dma((2 * KCH,)), dma((5,)), dma, dma, dma((2,)), dma((2,)), dma((2,)), dma((2,)),
                 dma, dma, dma, dma, dma, dma, dma, dma, dma, dma, dma, dma,
             ],
             compiler_params=pltpu.CompilerParams(collective_id=0, has_side_effects=True,

time: 45.3 us -> 46 us (1.015)
  Pallas kernels: 44.5 us -> 45.2 us
    pallas_call x1, Pallas kernels: 41.6 us -> 42.3 us  [local_step(): pl.pallas_call(main_kernel, name='decode', out_shape=(jax.ShapeDtypeStruc...]
where the time goes in v4:
time: 46 us; the launch traced here: 45.9 us
  Pallas kernels  45.2 us (98%)
  between operations  0.66 us (1%)
    pallas_call x1, Pallas kernels, local_step(): pl.pallas_call(main_kernel, name='decode', out_shape=(jax.ShapeDtypeStruc...  42.3 us
    pallas_call x1, Pallas kernels, local_step(): pl.pallas_call(update_kernel, name='update', out_shape=(jax.ShapeDtypeStr...  2.9 us

profile of v4, /device:TPU:1, one launch (start us, length us, event | category | flops | bytes accessed | tf_op | source)
XLA Modules:
  0.0 45.9 jit_solution(957927880460415376)
XLA Ops:
  0.6 0.0 copy-start
  0.6 42.3 %decode.1 = (bf16[2,64,8,128]{3,2,1,0:T(8,128)(2,1)S(1)}, bf16[2,2,8,8,128]{4,3,2,1,0:T(8,128)(2,1)S(1)}, bf16[16,512,128]{2,1,0:T(8,128)(2,1)S(1)}, bf16[16,512,128]{2,1,0:T(8,128)(2,1)S(1)}) custom-call(s32[16]{0:T(128)} %pos_ref.1, bf16[16,8192]{1,0:T(8,128)(2,1)} %x_hbm.1, bf16[8192,8192]{1,0:T(8,128)(2,1)} %wq_ref.1, bf16[8192,1024]{1,0:T(8,128)(2,1)} %wk_ref.1, ...), custom_call_target="tpu_custom_call" | custom-call | tf_op jit(solution)/shard_map/decode/pallas_call | solution.py:349
  43.0 0.0 copy-done
  43.0 2.9 %update.1 = (bf16[2,64,8,128]{3,2,1,0:T(8,128)(2,1)}, bf16[16,64,8,128]{3,2,1,0:T(8,128)(2,1)}, bf16[16,64,8,128]{3,2,1,0:T(8,128)(2,1)}) custom-call(s32[16]{0:T(128)S(1)} %copy-done, bf16[2,16,8,128]{3,2,1,0:T(8,128)(2,1)S(1)} %bitcast.10, bf16[2,64,8,128]{3,2,1,0:T(8,128)(2,1)S(1)} %get-tuple-element.11.y_ref, bf16[16,64,8,128]{3,2,1,0:T(8,128)(2,1)S(1)} %bitcast.8, ...), custom_call_target="tpu_custom_call" | custom-call | tf_op jit(solution)/shard_map/update/pallas_call | solution.py:377
Async XLA Ops:
  0.6 42.3 %copy-start = (s32[16]{0:T(128)S(1)}, s32[16]{0:T(128)}, u32[]{:S(2)}) copy-start(s32[16]{0:T(128)} %pos_ref.1) | copy-start | bytes 196

commit v5 on v4

--- a/solution.py
+++ b/solution.py
@@ -10,6 +10,7 @@
 F32 = jnp.float32
 MESH = pl.DeviceIdType.MESH
 DECODE_VMEM = 40
+LATE = 4
 KCH = 8
 RING = (0, 1, 2, 1)
 
@@ -40,8 +41,8 @@
 
 def main_kernel(pos_hbm, x_hbm, wq_ref, wk_ref, wv_ref, wo_ref, k_ref, v_ref,
                 y_ref, kvnew_ref, km_ref, vm_ref,
-                pos_ref, x_ref, wqb, wkvb, kbuf, vbuf, wob, qsend, qrecv, kvsend, kvrecv, kvf, qf, colidx,
-                opart, opeer, speer, oown, osend, orecv, ssend, srecv, ysend, yrecv, yb, yg,
+                pos_ref, x_ref, wqb, wkvb, kbuf, kt, vbuf, wob, qsend, qrecv, kvsend, kvrecv, kvf, qf, colidx,
+                opart, opeer, speer, oown, osum, osend, orecv, ssend, srecv, ysend, yrecv, yb, yg,
                 ring_sem, xsem, wsem, ksem, dw_send, dw_recv, d2d_send, d2d_recv, q_send, q_recv, o_send, o_recv,
                 s_send, s_recv, ys_send, ys_recv, yg_send, yg_recv, pp_send, pp_recv, pn_send, pn_recv):
     me = lax.axis_index("seq")
@@ -54,8 +55,10 @@
     def dev(d):
         return {"seq": d}
 
+    zs, ys, xs = ([((c + i) % 4) * n for i in range(4)] for c, n in ((cz, 16), (cy, 4), (cx, 1)))
+
     def chip_at(o):
-        return ((cz + o[0]) % 4) * 16 + ((cy + o[1]) % 4) * 4 + (cx + o[2]) % 4
+        return zs[o[0]] + ys[o[1]] + xs[o[2]]
 
     rows = 8192 // KCH
     qcol = pl.multiple_of(slot * 256, 256)
@@ -120,7 +123,8 @@
             loc[1].start()
         accq = accq + jnp.dot(x_ref[:, i * rows:(i + 1) * rows], wqb[i * rows:(i + 1) * rows, :],
                               preferred_element_type=F32)
-    qsend[...] = accq.astype(BF16)
+    for h in range(2):
+        qsend[h] = accq[h * 8:h * 8 + 8].astype(BF16)
     loc[2].start()
     pl.semaphore_wait(bar, 31)
     greet(2)
@@ -155,45 +159,53 @@
 
     greeted(2)
     greet(1)
+    loc[0].wait()
+    for b in range(16):
+        kt[b] = kbuf[b].T
     greeted(1)
     greet(0)
     wait_all(qrecv.at[pl.ds(0, 31)], q_recv.at[0])
     dw = rcopy(wo_ref, wob.at[core], dw_send, dw_recv, partner)
     dw.start()
-    for s in range(32):
-        q8 = qrecv[s].astype(F32)
-        for j in range(2):
-            qf[:, s * 2 + j, :] = q8[:, j * 128:(j + 1) * 128]
-    loc[0].wait()
+
+    def spread_q(half):
+        for s in range(32):
+            q8 = qrecv[s, half].astype(F32)
+            for j in range(2):
+                qf[half, pl.ds((s * 2 + j) * 8, 8), :] = q8[:, j * 128:(j + 1) * 128]
+
     loc[1].wait()
-
     lane = lax.broadcasted_iota(jnp.int32, (64, 128), 1)
     scale = 128 ** -0.5
     neg = -jnp.inf
 
-    def attend(half, dst):
-        stats = jnp.zeros((64, 128), F32)
-        for i in range(8):
+    def attend(half, dst, mst, lst, which):
+        for i in which:
             b = half * 8 + i
             pos = pos_ref[b]
-            qb = qf[b]
-            s = lax.dot_general(qb.astype(BF16), kbuf[b], (((1,), (1,)), ((), ())),
-                                preferred_element_type=F32) * scale
+            qb = qf[half, pl.ds(i, 64, stride=8), :]
+            s = jnp.dot(qb.astype(BF16), kt[b], preferred_element_type=F32) * scale
             s = jnp.where(colidx[...] < pos, s, neg)
             m = jnp.max(s, axis=1, keepdims=True)
             p = jnp.exp(s - jnp.where(m == neg, 0.0, m))
             l = jnp.sum(p, axis=1, keepdims=True)
             dst[i] = jnp.dot(p.astype(BF16), vbuf[b], preferred_element_type=F32)
-            stats = jnp.where(lane == i, m, stats)
-            stats = jnp.where(lane == 8 + i, l, stats)
-        return stats
-
-    ssend[:, 0, :] = attend(other, opart)
+            mst = jnp.where(lane == i, m, mst)
+            lst = jnp.where(lane == i, l, lst)
+        return mst, lst
+
+    def pack(m, l):
+        return jnp.where(lane < 8, m, pltpu.roll(l, 8, 1))
+
+    spread_q(other)
+    none = jnp.zeros((64, 128), F32)
+    ssend[:, 0, :] = pack(*attend(other, opart, none, none, range(8)))
+    spread_q(core)
     do = [rcopy(opart, opeer, d2d_send.at[0], d2d_recv.at[0], partner),
           rcopy(ssend, speer, d2d_send.at[1], d2d_recv.at[1], partner)]
     for c in do:
         c.start()
-    st1 = attend(core, oown)
+    m1, l1 = attend(core, oown, none, none, range(LATE))
 
     @pl.when(core == 0)
     def _():
@@ -212,22 +224,23 @@
     do[1].wait()
     st2 = speer[:, 0, :]
     do[0].wait()
-    stats = jnp.zeros((64, 128), F32)
+    m1, l1 = attend(core, oown, m1, l1, range(LATE, 8))
+    m2, l2, m3 = st2, pltpu.roll(st2, 120, 1), none
     for i in range(8):
-        m1, m2 = st1[:, i:i + 1], st2[:, i:i + 1]
-        l1, l2 = st1[:, 8 + i:9 + i], st2[:, 8 + i:9 + i]
         kn = jnp.broadcast_to(kvf[0, core, i][:, None, :], (8, 8, 128)).reshape(64, 128)
+        snew = jnp.sum(qf[core, pl.ds(i, 64, stride=8), :] * kn, axis=1, keepdims=True) * scale
+        here = jnp.full((64, 1), pos_ref[core * 8 + i] // 128, jnp.int32) == chip
+        m3 = jnp.where(lane == i, jnp.where(here, snew, neg), m3)
+    m = jnp.maximum(jnp.maximum(m1, m2), m3)
+    msafe = jnp.where(m == neg, 0.0, m)
+    w1, w2, w3 = jnp.exp(m1 - msafe), jnp.exp(m2 - msafe), jnp.exp(m3 - msafe)
+    stats = pack(m, w1 * l1 + w2 * l2 + w3)
+    for i in range(8):
         vn = jnp.broadcast_to(kvf[1, core, i][:, None, :], (8, 8, 128)).reshape(64, 128)
-        snew = jnp.sum(qf[core * 8 + i] * kn, axis=1, keepdims=True) * scale
-        here = jnp.full((64, 1), pos_ref[core * 8 + i] // 128, jnp.int32) == chip
-        snew = jnp.where(here, snew, neg)
-        m = jnp.maximum(jnp.maximum(m1, m2), snew)
-        msafe = jnp.where(m == neg, 0.0, m)
-        w1, w2, w3 = jnp.exp(m1 - msafe), jnp.exp(m2 - msafe), jnp.exp(snew - msafe)
-        osend[:, i, :] = w1 * oown[i] + w2 * opeer[i] + w3 * vn
-        stats = jnp.where(lane == i, m, stats)
-        stats = jnp.where(lane == 8 + i, w1 * l1 + w2 * l2 + w3, stats)
+        osum[pl.ds(i * 64, 64), :] = (w1[:, i:i + 1] * oown[i] + w2[:, i:i + 1] * opeer[i] + w3[:, i:i + 1] * vn)
     ssend[:, 0, :] = stats
+    for h in range(64):
+        osend[h] = osum[pl.ds(h, 8, stride=64), :]
 
     greeted(0)
 
@@ -356,14 +369,14 @@
             scratch_shapes=[
                 pltpu.SMEM((16,), jnp.int32), pltpu.VMEM((16, 8192), BF16),
                 pltpu.VMEM((8192, 256), BF16), pltpu.VMEM((8192, 128), BF16),
-                pltpu.VMEM((16, 512, 128), BF16), pltpu.VMEM((16, 512, 128), BF16),
-                pltpu.VMEM((2, 64, 8192), BF16),
-                pltpu.VMEM((16, 256), BF16), pltpu.VMEM((32, 16, 256), BF16),
+                pltpu.VMEM((16, 512, 128), BF16), pltpu.VMEM((16, 128, 512), BF16),
+                pltpu.VMEM((16, 512, 128), BF16), pltpu.VMEM((2, 64, 8192), BF16),
+                pltpu.VMEM((2, 8, 256), BF16), pltpu.VMEM((32, 2, 8, 256), BF16),
                 pltpu.VMEM((2, 8, 128), BF16), pltpu.VMEM((16, 2, 8, 128), BF16),
-                pltpu.VMEM((2, 2, 8, 8, 128), F32), pltpu.VMEM((16, 64, 128), F32),
+                pltpu.VMEM((2, 2, 8, 8, 128), F32), pltpu.VMEM((2, 512, 128), F32),
                 pltpu.VMEM((64, 512), jnp.int32),
                 pltpu.VMEM((8, 64, 128), F32), pltpu.VMEM((8, 64, 128), F32),
-                pltpu.VMEM((64, 1, 128), F32), pltpu.VMEM((8, 64, 128), F32),
+                pltpu.VMEM((64, 1, 128), F32), pltpu.VMEM((8, 64, 128), F32), pltpu.VMEM((512, 128), F32),
                 pltpu.VMEM((64, 8, 128), F32), pltpu.VMEM((64, 8, 128), F32),
                 pltpu.VMEM((64, 1, 128), F32), pltpu.VMEM((64, 1, 128), F32),
                 pltpu.VMEM((64, 8, 128), F32), pltpu.VMEM((64, 8, 128), F32),

time: 46 us -> 44.9 us (0.976)
  Pallas kernels: 45.2 us -> 44.2 us
    pallas_call x1, Pallas kernels: 42.3 us -> 41.3 us  [local_step(): pl.pallas_call(main_kernel, name='decode', out_shape=(jax.ShapeDtypeStruc...]
where the time goes in v5:
time: 44.9 us; the launch traced here: 44.8 us
  Pallas kernels  44.2 us (98%)
  between operations  0.66 us (1%)
    pallas_call x1, Pallas kernels, local_step(): pl.pallas_call(main_kernel, name='decode', out_shape=(jax.ShapeDtypeStruc...  41.3 us
    pallas_call x1, Pallas kernels, local_step(): pl.pallas_call(update_kernel, name='update', out_shape=(jax.ShapeDtypeStr...  2.9 us

profile of v5, /device:TPU:1, one launch (start us, length us, event | category | flops | bytes accessed | tf_op | source)
XLA Modules:
  0.0 44.8 jit_solution(12038388332992086205)
XLA Ops:
  0.6 0.0 copy-start
  0.6 41.3 %decode.1 = (bf16[2,64,8,128]{3,2,1,0:T(8,128)(2,1)S(1)}, bf16[2,2,8,8,128]{4,3,2,1,0:T(8,128)(2,1)S(1)}, bf16[16,512,128]{2,1,0:T(8,128)(2,1)S(1)}, bf16[16,512,128]{2,1,0:T(8,128)(2,1)S(1)}) custom-call(s32[16]{0:T(128)} %pos_ref.1, bf16[16,8192]{1,0:T(8,128)(2,1)} %x_hbm.1, bf16[8192,8192]{1,0:T(8,128)(2,1)} %wq_ref.1, bf16[8192,1024]{1,0:T(8,128)(2,1)} %wk_ref.1, ...), custom_call_target="tpu_custom_call" | custom-call | tf_op jit(solution)/shard_map/decode/pallas_call | solution.py:362
  41.9 0.0 copy-done
  41.9 2.9 %update.1 = (bf16[2,64,8,128]{3,2,1,0:T(8,128)(2,1)}, bf16[16,64,8,128]{3,2,1,0:T(8,128)(2,1)}, bf16[16,64,8,128]{3,2,1,0:T(8,128)(2,1)}) custom-call(s32[16]{0:T(128)S(1)} %copy-done, bf16[2,16,8,128]{3,2,1,0:T(8,128)(2,1)S(1)} %bitcast.10, bf16[2,64,8,128]{3,2,1,0:T(8,128)(2,1)S(1)} %get-tuple-element.11.y_ref, bf16[16,64,8,128]{3,2,1,0:T(8,128)(2,1)S(1)} %bitcast.8, ...), custom_call_target="tpu_custom_call" | custom-call | tf_op jit(solution)/shard_map/update/pallas_call | solution.py:390
Async XLA Ops:
  0.6 41.3 %copy-start = (s32[16]{0:T(128)S(1)}, s32[16]{0:T(128)}, u32[]{:S(2)}) copy-start(s32[16]{0:T(128)} %pos_ref.1) | copy-start | bytes 196
